TPU v7x, 32 devices: a whole 2x2x4 slice. The times are simulated.
32 devices in a mesh: row: 4 (over y, core), col: 8 (over z, x).
Axes of the slice: x: 2, y: 2, z: 4, core: 2. Of those that a mesh axis runs over, the one named last changes fastest.
Arguments:
- u_state: float32 [2048, 128], P(('row', 'col')), may hold values from -12 to 12
- v_state: float32 [3, 2048, 128], P(None, ('col', 'row')), may hold values from -12 to 12
- alpha_prev: float32 [128], replicated, may hold values from 0.5 to 2
- near_blocks: bfloat16 [4, 8, 16, 128, 3, 128], P('row', 'col'), may hold values from -0.3125 to 0.3125
- near_rows: int32 [4, 8, 16], P('row', 'col'), may hold values from 0 to 3
- near_cols: int32 [4, 8, 16], P('row', 'col'), may hold values from 0 to 1
- near_count: int32 [4, 8], P('row', 'col'), may hold values from 4 to 16, as said below
- mid_left: bfloat16 [8, 64, 2048], P('col', None, 'row'), may hold values from -0.75 to 0.75
- mid_right: bfloat16 [4, 64, 3, 2048], P('row', None, None, 'col'), may hold values from -0.21875 to 0.21875
- mid_rank: int32 [4, 8], P('row', 'col'), may hold values from 32 to 64
- coarse_left: bfloat16 [8, 32, 2048], P('col', None, 'row'), may hold values from -1 to 1
- coarse_right: bfloat16 [32, 3, 2048], P(None, None, ('col', 'row')), may hold values from -0.21875 to 0.21875
- coarse_rank: int32 [8], P('col'), may hold values from 16 to 32
Outputs:
- u_next: float32 [2048, 128], P(('row', 'col'))
- v_next: float32 [3, 2048, 128], P(None, ('col', 'row'))
- norms: float32 [2, 128], replicated
Inputs may be any that keep to these rules, and one draw needn't show every extreme that they name: Slots 0 to near_count - 1 of a block are live; some block has all 16 slots live.
All inputs are finite; a program needn't handle non-finite values.
Results may differ from a plain program's by a relative error of at most 0.0044.
Values may be sent and summed in bfloat16 or wider, within the bound.
A program may use at most 64 MiB of HBM per device.

v0:
```python
import functools

import jax
import jax.numpy as jnp
from jax import lax
from jax.experimental import pallas as pl
from jax.experimental.pallas import tpu as pltpu
from jax.sharding import PartitionSpec as P

tiny_add = 1e-06
MESH = pl.DeviceIdType.MESH
f32, bf16 = jnp.float32, jnp.bfloat16


def fold(values):
    return (values * values).reshape(values.shape[0] // 8, 8, values.shape[1]).sum(axis=0)


def turn(values):
    return jnp.transpose(values.astype(f32), (1, 0))


def kernel(
    sizes,
    rows_hbm,
    cols_hbm,
    count_smem,
    mid_rank_smem,
    coarse_rank_smem,
    u_hbm,
    v_hbm,
    alpha_hbm,
    near_hbm,
    mid_left_hbm,
    mid_right_hbm,
    coarse_left_hbm,
    coarse_right_hbm,
    u_out,
    v_out,
    beta_out,
    vsq_row,
    rows_smem,
    cols_smem,
    near,
    u_old,
    v_old,
    alpha_old,
    left,
    left_turned,
    right,
    slip,
    coarse_all,
    acc,
    fsend,
    frecv,
    ug,
    ut,
    sq,
    back_acc,
    bsend,
    brecv,
    vsq_col,
    near_sem,
    in_sem,
    slip_send,
    slip_recv,
    coarse_send,
    coarse_recv,
    f_send,
    f_recv,
    u_send,
    u_recv,
    sq_send,
    sq_recv,
    b_send,
    b_recv,
    vc_send,
    vc_recv,
    vr_send,
    vr_recv,
):
    n_row, n_col, unroll = sizes
    me_r, me_c = lax.axis_index("row"), lax.axis_index("col")
    slots, _, clp, clq = near.shape
    pt, rhs = u_old.shape
    pd = v_old.shape[1]
    km, kc = mid_left_hbm.shape[0], coarse_left_hbm.shape[0]
    kt = km + 2 * kc
    row_groups, col_groups = acc.shape[0], back_acc.shape[0]
    per_row, per_col = clp // pt, clq // pd

    def row_peer(step):
        return lax.rem(me_r + step, n_row)

    def far_first(me, count, step):
        upper = me >= count // 2
        own = jnp.where(upper, me, count - 1 - me)
        place = step - 1 + (step - 1 >= own).astype(jnp.int32)
        return jnp.where(upper, place, count - 1 - place)

    def col_peer(step):
        return far_first(me_c, n_col, step)

    barrier = pltpu.get_barrier_semaphore()
    for step in range(1, n_row):
        pl.semaphore_signal(barrier, device_id={"row": row_peer(step)}, device_id_type=MESH)
    for step in range(1, n_col):
        pl.semaphore_signal(barrier, device_id={"col": col_peer(step)}, device_id_type=MESH)

    loads = [
        pltpu.make_async_copy(src, dst, in_sem.at[place])
        for place, (src, dst) in enumerate(
            [
                (v_hbm, v_old),
                (coarse_right_hbm, coarse_all.at[me_r]),
                (mid_right_hbm, right.at[:, 0:km, :]),
                (mid_left_hbm, left.at[0:km, :]),
                (coarse_left_hbm, left.at[km : km + kc, :]),
                (coarse_left_hbm, left.at[km + kc : kt, :]),
                (u_hbm, u_old),
                (alpha_hbm, alpha_old),
                (rows_hbm, rows_smem),
                (cols_hbm, cols_smem),
            ]
        )
    ]
    for load in loads:
        load.start()

    def near_load(slot):
        return pltpu.make_async_copy(near_hbm.at[slot], near.at[slot], near_sem.at[slot])

    for slot in range(slots):
        near_load(slot).start()

    def exchange(axis, me, count, peer, source, target, send_sem, recv_sem):
        copies = [
            pltpu.make_async_remote_copy(
                src_ref=source(peer(step)),
                dst_ref=target,
                send_sem=send_sem.at[step - 1],
                recv_sem=recv_sem.at[me],
                device_id={axis: peer(step)},
                device_id_type=MESH,
            )
            for step in range(1, count)
        ]
        for copy in copies:
            copy.start()
        incoming = [
            pltpu.make_async_remote_copy(
                src_ref=source(peer(step)),
                dst_ref=target,
                send_sem=send_sem.at[step - 1],
                recv_sem=recv_sem.at[peer(step)],
                device_id={axis: peer(step)},
                device_id_type=MESH,
            )
            for step in range(1, count)
        ]
        return copies, incoming

    def across_rows(source, target, send_sem, recv_sem):
        return exchange("row", me_r, n_row, row_peer, source, target, send_sem, recv_sem)

    def across_cols(source, target, send_sem, recv_sem):
        return exchange("col", me_c, n_col, col_peer, source, target, send_sem, recv_sem)

    def arrived(copies):
        for copy in copies[1]:
            copy.wait_recv()

    loads[0].wait()
    slip[me_r] = v_old[...].astype(bf16)
    loads[1].wait()
    pl.semaphore_wait(barrier, n_row + n_col - 2)
    sent_slip = across_rows(lambda peer: slip.at[me_r], slip.at[me_r], slip_send, slip_recv)
    sent_coarse = across_rows(
        lambda peer: coarse_all.at[me_r], coarse_all.at[me_r], coarse_send, coarse_recv
    )
    for load in loads[2:]:
        load.wait()
    for group in range(row_groups):
        span = slice(group * clp, (group + 1) * clp)
        left_turned[span, :] = turn(left[:, span]).astype(bf16)
    acc[...] = jnp.zeros_like(acc)
    back_acc[...] = jnp.zeros_like(back_acc)
    arrived(sent_slip)

    def forward_steps(turn_index, carry):
        products, weights = [], []
        for inner in range(unroll):
            slot = turn_index * unroll + inner
            near_load(slot).wait()
            first = cols_smem[0, 0, slot] * per_col
            total = None
            for k in range(3):
                picked = slip[pl.ds(first, per_col), k].reshape(clq, rhs)
                term = jnp.dot(near[slot, k], picked, preferred_element_type=f32)
                total = term if total is None else total + term
            products.append(total)
            live = slot < count_smem[0, 0]
            weights.append(
                [
                    jnp.where(jnp.logical_and(rows_smem[0, 0, slot] == group, live), 1.0, 0.0).astype(f32)
                    for group in range(row_groups)
                ]
            )
        for group in range(row_groups):
            value = acc[group]
            for inner in range(unroll):
                value = value + products[inner] * weights[inner][group]
            acc[group] = value
        return carry

    lax.fori_loop(0, slots // unroll, forward_steps, 0)

    arrived(sent_coarse)
    for peer in range(n_row):
        for k in range(3):
            piece = coarse_all[peer, k]
            right[k, km : km + kc, peer * pd : (peer + 1) * pd] = piece
            right[k, km + kc : kt, peer * pd : (peer + 1) * pd] = piece
    codes = jnp.zeros((kt, rhs), f32)
    for k in range(3):
        codes = codes + jnp.dot(
            right[k], slip[:, k].reshape(n_row * pd, rhs), preferred_element_type=f32
        )
    place = lax.broadcasted_iota(jnp.int32, (kt, rhs), 0)
    limit = jnp.where(place < km, mid_rank_smem[0, 0], coarse_rank_smem[0])
    inside = jnp.where(place < km, place, jnp.where(place < km + kc, place - km, kt))
    codes = jnp.where(inside < limit, codes, 0.0).astype(bf16)
    for group in range(row_groups):
        span = slice(group * clp, (group + 1) * clp)
        value = acc[group] + jnp.dot(left_turned[span, :], codes, preferred_element_type=f32)
        fsend[group * per_row : (group + 1) * per_row] = value.astype(bf16).reshape(
            per_row, pt, rhs
        )
    sent_f = across_cols(lambda peer: fsend.at[peer], frecv.at[me_c], f_send, f_recv)
    frecv[me_c] = fsend[me_c]
    arrived(sent_f)
    u_hat = -alpha_old[...] * u_old[...]
    for peer in range(n_col):
        u_hat = u_hat + frecv[peer].astype(f32)
    ug[me_c] = u_hat.astype(bf16)
    sent_u = across_cols(lambda peer: ug.at[me_c], ug.at[me_c], u_send, u_recv)
    u_old[...] = u_hat
    arrived(sent_u)

    squares = jnp.zeros((8, rhs), f32)
    for group in range(row_groups):
        value = ug[group * per_row : (group + 1) * per_row].reshape(clp, rhs).astype(f32)
        squares = squares + fold(value)
        ut[group] = jnp.transpose(value, (1, 0)).astype(bf16)
    sq[me_r] = squares
    sent_sq = across_rows(lambda peer: sq.at[me_r], sq.at[me_r], sq_send, sq_recv)

    def backward_steps(turn_index, carry):
        products, weights = [], []
        for inner in range(unroll):
            slot = turn_index * unroll + inner
            picked = ut[rows_smem[0, 0, slot]]
            products.append(
                [jnp.dot(picked, near[slot, k], preferred_element_type=f32) for k in range(3)]
            )
            live = slot < count_smem[0, 0]
            weights.append(
                [
                    jnp.where(jnp.logical_and(cols_smem[0, 0, slot] == group, live), 1.0, 0.0).astype(f32)
                    for group in range(col_groups)
                ]
            )
        for group in range(col_groups):
            for k in range(3):
                value = back_acc[group, k]
                for inner in range(unroll):
                    value = value + products[inner][k] * weights[inner][group]
                back_acc[group, k] = value
        return carry

    lax.fori_loop(0, slots // unroll, backward_steps, 0)

    loads_turned = jnp.zeros((rhs, kt), f32)
    for group in range(row_groups):
        loads_turned = loads_turned + jnp.dot(
            ut[group],
            left_turned[group * clp : (group + 1) * clp, :],
            preferred_element_type=f32,
        )
    place = lax.broadcasted_iota(jnp.int32, (rhs, kt), 1)
    limit = jnp.where(place < km, mid_rank_smem[0, 0], coarse_rank_smem[0])
    inside = jnp.where(place < km, place, jnp.where(place < km + kc, place - km, place - km - kc))
    loads_turned = jnp.where(inside < limit, loads_turned, 0.0)
    high = loads_turned.astype(bf16)
    low = (loads_turned - high.astype(f32)).astype(bf16)
    factors = jnp.where(place < km + kc, high.astype(f32), low.astype(f32)).astype(bf16)
    for group in range(col_groups):
        for k in range(3):
            value = back_acc[group, k] + jnp.dot(
                factors,
                right[k, :, group * clq : (group + 1) * clq],
                preferred_element_type=f32,
            )
            value = jnp.transpose(value, (1, 0)).astype(bf16).reshape(per_col, pd, rhs)
            bsend[group * per_col : (group + 1) * per_col, k] = value
    sent_b = across_rows(lambda peer: bsend.at[peer], brecv.at[me_r], b_send, b_recv)
    brecv[me_r] = bsend[me_r]
    arrived(sent_sq)
    square_sum = jnp.zeros((8, rhs), f32)
    for peer in range(n_row):
        square_sum = square_sum + sq[peer]
    points = pt * n_row * n_col
    beta = jnp.sqrt(jnp.sum(square_sum, axis=0, keepdims=True) / points + tiny_add)
    beta_out[...] = beta
    u_out[...] = u_old[...] / beta
    arrived(sent_b)
    v_squares = jnp.zeros((8, rhs), f32)
    for k in range(3):
        total = jnp.zeros((pd, rhs), f32)
        for peer in range(n_row):
            total = total + brecv[peer, k].astype(f32)
        v_hat = total / beta - beta * v_old[k]
        v_out[k] = v_hat
        v_squares = v_squares + fold(v_hat)
    vsq_col[me_c] = v_squares
    sent_vc = across_cols(lambda peer: vsq_col.at[me_c], vsq_col.at[me_c], vc_send, vc_recv)
    arrived(sent_vc)
    v_squares = jnp.zeros((8, rhs), f32)
    for peer in range(n_col):
        v_squares = v_squares + vsq_col[peer]
    vsq_row[me_r] = v_squares
    sent_vr = across_rows(lambda peer: vsq_row.at[me_r], vsq_row.at[me_r], vr_send, vr_recv)
    arrived(sent_vr)
    for copies in (sent_slip, sent_coarse, sent_f, sent_u, sent_sq, sent_b, sent_vc, sent_vr):
        for copy in copies[0]:
            copy.wait_send()


def finish(unknowns, u_ref, v_ref, beta_ref, squares_ref, u_out, v_out, norms_out):
    total = jnp.zeros(squares_ref.shape[1:], f32)
    for peer in range(squares_ref.shape[0]):
        total = total + squares_ref[peer]
    alpha = jnp.sqrt(jnp.sum(total, axis=0, keepdims=True) / unknowns + tiny_add)
    norms_out[0:1, :] = beta_ref[...]
    norms_out[1:2, :] = alpha
    u_out[...] = u_ref[...]
    v_out[...] = v_ref[...] / alpha


def per_device(
    n_row,
    n_col,
    u_state,
    v_state,
    alpha_prev,
    near_blocks,
    near_rows,
    near_cols,
    near_count,
    mid_left,
    mid_right,
    mid_rank,
    coarse_left,
    coarse_right,
    coarse_rank,
):
    slots, clp, _, clq = near_blocks.shape[2:]
    pt, rhs = u_state.shape
    pd = v_state.shape[1]
    km, kc = mid_left.shape[1], coarse_left.shape[1]
    kt = km + 2 * kc
    row_span, col_span = mid_left.shape[2], mid_right.shape[3]
    row_groups, col_groups = row_span // clp, col_span // clq
    unroll = 16 if slots % 16 == 0 else 1
    smem = pl.BlockSpec(memory_space=pltpu.SMEM)
    in_hbm = pl.BlockSpec(memory_space=pltpu.HBM)
    vmem = pl.BlockSpec(memory_space=pltpu.VMEM)
    dma = pltpu.SemaphoreType.DMA
    row_sem, col_sem = dma((n_row,)), dma((n_col,))
    scratch = [
        pltpu.SMEM(near_rows.shape, jnp.int32),
        pltpu.SMEM(near_cols.shape, jnp.int32),
        pltpu.VMEM((slots, 3, clp, clq), bf16),
        pltpu.VMEM((pt, rhs), f32),
        pltpu.VMEM((3, pd, rhs), f32),
        pltpu.VMEM((1, rhs), f32),
        pltpu.VMEM((kt, row_span), bf16),
        pltpu.VMEM((row_span, kt), bf16),
        pltpu.VMEM((3, kt, col_span), bf16),
        pltpu.VMEM((n_row, 3, pd, rhs), bf16),
        pltpu.VMEM((n_row, 3, kc, pd), bf16),
        pltpu.VMEM((row_groups, clp, rhs), f32),
        pltpu.VMEM((n_col, pt, rhs), bf16),
        pltpu.VMEM((n_col, pt, rhs), bf16),
        pltpu.VMEM((n_col, pt, rhs), bf16),
        pltpu.VMEM((row_groups, rhs, clp), bf16),
        pltpu.VMEM((n_row, 8, rhs), f32),
        pltpu.VMEM((col_groups, 3, rhs, clq), f32),
        pltpu.VMEM((n_row, 3, pd, rhs), bf16),
        pltpu.VMEM((n_row, 3, pd, rhs), bf16),
        pltpu.VMEM((n_col, 8, rhs), f32),
        dma((slots,)),
        dma((10,)),
        row_sem,
        row_sem,
        row_sem,
        row_sem,
        col_sem,
        col_sem,
        col_sem,
        col_sem,
        row_sem,
        row_sem,
        row_sem,
        row_sem,
        col_sem,
        col_sem,
        row_sem,
        row_sem,
    ]
    held = pl.pallas_call(
        functools.partial(kernel, (n_row, n_col, unroll)),
        out_shape=(
            pltpu.VMEM((pt, rhs), f32),
            pltpu.VMEM((3, pd, rhs), f32),
            pltpu.VMEM((1, rhs), f32),
            pltpu.VMEM((n_row, 8, rhs), f32),
        ),
        in_specs=[in_hbm] * 2 + [smem] * 3 + [in_hbm] * 8,
        out_specs=(vmem,) * 4,
        scratch_shapes=scratch,
        compiler_params=pltpu.CompilerParams(
            collective_id=0, has_side_effects=True, vmem_limit_bytes=60 * 1024 * 1024
        ),
        name="lsqr",
    )(
        near_rows,
        near_cols,
        near_count,
        mid_rank,
        coarse_rank,
        u_state,
        v_state,
        alpha_prev.reshape(1, rhs),
        jnp.transpose(near_blocks[0, 0], (0, 2, 1, 3)),
        mid_left[0],
        jnp.transpose(mid_right[0], (1, 0, 2)),
        coarse_left[0],
        jnp.transpose(coarse_right, (1, 0, 2)),
    )
    return pl.pallas_call(
        functools.partial(finish, 3 * pd * n_row * n_col),
        out_shape=(
            jax.ShapeDtypeStruct((pt, rhs), f32),
            jax.ShapeDtypeStruct((3, pd, rhs), f32),
            jax.ShapeDtypeStruct((2, rhs), f32),
        ),
        in_specs=[vmem] * 4,
        out_specs=(vmem,) * 3,
        name="finish",
    )(*[pltpu.with_memory_space_constraint(value, pltpu.VMEM) for value in held])


def solution(mesh):
    placed = (
        P(("row", "col"), None),
        P(None, ("col", "row"), None),
        P(),
        P("row", "col", None, None, None, None),
        P("row", "col", None),
        P("row", "col", None),
        P("row", "col"),
        P("col", None, "row"),
        P("row", None, None, "col"),
        P("row", "col"),
        P("col", None, "row"),
        P(None, None, ("col", "row")),
        P("col"),
    )
    return jax.shard_map(
        functools.partial(per_device, mesh.shape["row"], mesh.shape["col"]),
        mesh=mesh,
        in_specs=placed,
        out_specs=(P(("row", "col"), None), P(None, ("col", "row"), None), P()),
        check_vma=False,
    )
```

profile of v0, /device:TPU:0, one launch (start us, length us, event | category | flops | bytes accessed | tf_op | source)
XLA Modules:
  0.0 38.2 jit_solution(10887985917619715121)
XLA Ops:
  2.6 34.9 %lsqr.1 = (f32[64,128]{1,0:T(8,128)S(1)}, f32[3,64,128]{2,1,0:T(8,128)S(1)}, f32[1,128]{1,0:T(1,128)S(1)}, f32[4,8,128]{2,1,0:T(8,128)S(1)}) custom-call(s32[1,1,16]{2,1,0:T(1,128)} %rows_hbm.1, s32[1,1,16]{2,1,0:T(1,128)} %cols_hbm.1, s32[1,1]{1,0:T(1,128)S(6)} %copy.16.count_smem, s32[1,1]{1,0:T(1,128)S(6)} %copy.17.mid_rank_smem, ...), custom_call_target="tpu_custom_call" | custom-call | tf_op jit(solution)/shard_map/lsqr/pallas_call | solution.py:421
  37.5 0.7 %finish.1 = (f32[64,128]{1,0:T(8,128)}, f32[3,64,128]{2,1,0:T(8,128)}, f32[2,128]{1,0:T(2,128)}) custom-call(f32[64,128]{1,0:T(8,128)S(1)} %get-tuple-element.7.u_ref, f32[3,64,128]{2,1,0:T(8,128)S(1)} %get-tuple-element.8.v_ref, f32[1,128]{1,0:T(1,128)S(1)} %get-tuple-element.9.beta_ref, f32[4,8,128]{2,1,0:T(8,128)S(1)} %get-tuple-element.10.squares_ref), custom_call_target="tpu_custom_call" | custom-call | tf_op jit(solution)/shard_map/finish/pallas_call | solution.py:451
where the time goes:
time: 38.3 us; the launch traced here: 38.2 us
  Pallas kernels  35.6 us (93%)
  between operations  2.58 us (7%)
    pallas_call x1, Pallas kernels, per_device(): pl.pallas_call(functools.partial(kernel, (n_row, n_col, unroll)), out_sha...  34.9 us

commit v1 on v0

--- a/solution.py
+++ b/solution.py
@@ -10,6 +10,7 @@
 tiny_add = 1e-06
 MESH = pl.DeviceIdType.MESH
 f32, bf16 = jnp.float32, jnp.bfloat16
+WHOLE_LIMIT = 64
 
 
 def fold(values):
@@ -24,9 +25,9 @@
     sizes,
     rows_hbm,
     cols_hbm,
-    count_smem,
-    mid_rank_smem,
-    coarse_rank_smem,
+    count_hbm,
+    mid_rank_hbm,
+    coarse_rank_hbm,
     u_hbm,
     v_hbm,
     alpha_hbm,
@@ -38,9 +39,12 @@
     u_out,
     v_out,
     beta_out,
-    vsq_row,
+    vsq_all,
     rows_smem,
     cols_smem,
+    count_smem,
+    mid_rank_smem,
+    coarse_rank_smem,
     near,
     u_old,
     v_old,
@@ -101,12 +105,6 @@
     def col_peer(step):
         return far_first(me_c, n_col, step)
 
-    barrier = pltpu.get_barrier_semaphore()
-    for step in range(1, n_row):
-        pl.semaphore_signal(barrier, device_id={"row": row_peer(step)}, device_id_type=MESH)
-    for step in range(1, n_col):
-        pl.semaphore_signal(barrier, device_id={"col": col_peer(step)}, device_id_type=MESH)
-
     loads = [
         pltpu.make_async_copy(src, dst, in_sem.at[place])
         for place, (src, dst) in enumerate(
@@ -121,17 +119,32 @@
                 (alpha_hbm, alpha_old),
                 (rows_hbm, rows_smem),
                 (cols_hbm, cols_smem),
+                (count_hbm, count_smem),
+                (mid_rank_hbm, mid_rank_smem),
+                (coarse_rank_hbm, coarse_rank_smem),
             ]
         )
     ]
-    for load in loads:
+    loads[0].start()
+    loads[1].start()
+
+    barrier = pltpu.get_barrier_semaphore()
+    whole = n_row * n_col <= WHOLE_LIMIT
+    if whole:
+        others = [(a, b) for b in range(n_col) for a in range(n_row)][1:]
+        spots = [(lax.rem(me_r + a, n_row), lax.rem(me_c + b, n_col)) for a, b in others]
+        for row, col in spots:
+            pl.semaphore_signal(barrier, device_id=(row, col), device_id_type=MESH)
+    else:
+        spots = [(row_peer(step), me_c) for step in range(1, n_row)]
+        spots += [(me_r, col_peer(step)) for step in range(1, n_col)]
+        for row, col in spots:
+            pl.semaphore_signal(barrier, device_id=(row, col), device_id_type=MESH)
+    for load in loads[2:]:
         load.start()
 
     def near_load(slot):
         return pltpu.make_async_copy(near_hbm.at[slot], near.at[slot], near_sem.at[slot])
-
-    for slot in range(slots):
-        near_load(slot).start()
 
     def exchange(axis, me, count, peer, source, target, send_sem, recv_sem):
         copies = [
@@ -173,11 +186,13 @@
     loads[0].wait()
     slip[me_r] = v_old[...].astype(bf16)
     loads[1].wait()
-    pl.semaphore_wait(barrier, n_row + n_col - 2)
+    pl.semaphore_wait(barrier, len(spots))
     sent_slip = across_rows(lambda peer: slip.at[me_r], slip.at[me_r], slip_send, slip_recv)
     sent_coarse = across_rows(
         lambda peer: coarse_all.at[me_r], coarse_all.at[me_r], coarse_send, coarse_recv
     )
+    for slot in range(slots):
+        near_load(slot).start()
     for load in loads[2:]:
         load.wait()
     for group in range(row_groups):
@@ -185,13 +200,14 @@
         left_turned[span, :] = turn(left[:, span]).astype(bf16)
     acc[...] = jnp.zeros_like(acc)
     back_acc[...] = jnp.zeros_like(back_acc)
+    for slot in range(slots):
+        near_load(slot).wait()
     arrived(sent_slip)
 
     def forward_steps(turn_index, carry):
         products, weights = [], []
         for inner in range(unroll):
             slot = turn_index * unroll + inner
-            near_load(slot).wait()
             first = cols_smem[0, 0, slot] * per_col
             total = None
             for k in range(3):
@@ -322,18 +338,42 @@
         v_hat = total / beta - beta * v_old[k]
         v_out[k] = v_hat
         v_squares = v_squares + fold(v_hat)
-    vsq_col[me_c] = v_squares
-    sent_vc = across_cols(lambda peer: vsq_col.at[me_c], vsq_col.at[me_c], vc_send, vc_recv)
-    arrived(sent_vc)
-    v_squares = jnp.zeros((8, rhs), f32)
-    for peer in range(n_col):
-        v_squares = v_squares + vsq_col[peer]
-    vsq_row[me_r] = v_squares
-    sent_vr = across_rows(lambda peer: vsq_row.at[me_r], vsq_row.at[me_r], vr_send, vr_recv)
-    arrived(sent_vr)
-    for copies in (sent_slip, sent_coarse, sent_f, sent_u, sent_sq, sent_b, sent_vc, sent_vr):
+    sent_v = []
+    if whole:
+        vsq_all[me_c, pl.ds(me_r, 1)] = jnp.sum(v_squares, axis=0, keepdims=True)
+
+        def row_sum(place, row, col):
+            return pltpu.make_async_remote_copy(
+                src_ref=vsq_all.at[me_c, pl.ds(me_r, 1)],
+                dst_ref=vsq_all.at[me_c, pl.ds(me_r, 1)],
+                send_sem=vc_send.at[place],
+                recv_sem=vc_recv.at[place],
+                device_id=(row, col),
+                device_id_type=MESH,
+            )
+
+        for place in reversed(range(len(spots))):
+            copy = row_sum(place, *spots[place])
+            copy.start()
+            sent_v.append(copy)
+        for copy in sent_v:
+            copy.wait_recv()
+    else:
+        vsq_col[me_c] = v_squares
+        sent_vc = across_cols(lambda peer: vsq_col.at[me_c], vsq_col.at[me_c], vc_send, vc_recv)
+        arrived(sent_vc)
+        v_squares = jnp.zeros((8, rhs), f32)
+        for peer in range(n_col):
+            v_squares = v_squares + vsq_col[peer]
+        vsq_all[me_r] = v_squares
+        sent_vr = across_rows(lambda peer: vsq_all.at[me_r], vsq_all.at[me_r], vr_send, vr_recv)
+        arrived(sent_vr)
+        sent_v = sent_vc[0] + sent_vr[0]
+    for copies in (sent_slip, sent_coarse, sent_f, sent_u, sent_sq, sent_b):
         for copy in copies[0]:
             copy.wait_send()
+    for copy in sent_v:
+        copy.wait_send()
 
 
 def finish(unknowns, u_ref, v_ref, beta_ref, squares_ref, u_out, v_out, norms_out):
@@ -372,14 +412,19 @@
     row_span, col_span = mid_left.shape[2], mid_right.shape[3]
     row_groups, col_groups = row_span // clp, col_span // clq
     unroll = 16 if slots % 16 == 0 else 1
-    smem = pl.BlockSpec(memory_space=pltpu.SMEM)
     in_hbm = pl.BlockSpec(memory_space=pltpu.HBM)
     vmem = pl.BlockSpec(memory_space=pltpu.VMEM)
     dma = pltpu.SemaphoreType.DMA
     row_sem, col_sem = dma((n_row,)), dma((n_col,))
+    whole = n_row * n_col <= WHOLE_LIMIT
+    last_sem = dma((n_row * n_col,)) if whole else col_sem
+    sums = (n_col, n_row, rhs) if whole else (n_row, 8, rhs)
     scratch = [
         pltpu.SMEM(near_rows.shape, jnp.int32),
         pltpu.SMEM(near_cols.shape, jnp.int32),
+        pltpu.SMEM(near_count.shape, jnp.int32),
+        pltpu.SMEM(mid_rank.shape, jnp.int32),
+        pltpu.SMEM(coarse_rank.shape, jnp.int32),
         pltpu.VMEM((slots, 3, clp, clq), bf16),
         pltpu.VMEM((pt, rhs), f32),
         pltpu.VMEM((3, pd, rhs), f32),
@@ -400,7 +445,7 @@
         pltpu.VMEM((n_row, 3, pd, rhs), bf16),
         pltpu.VMEM((n_col, 8, rhs), f32),
         dma((slots,)),
-        dma((10,)),
+        dma((13,)),
         row_sem,
         row_sem,
         row_sem,
@@ -413,8 +458,8 @@
         row_sem,
         row_sem,
         row_sem,
-        col_sem,
-        col_sem,
+        last_sem,
+        last_sem,
         row_sem,
         row_sem,
     ]
@@ -424,9 +469,9 @@
             pltpu.VMEM((pt, rhs), f32),
             pltpu.VMEM((3, pd, rhs), f32),
             pltpu.VMEM((1, rhs), f32),
-            pltpu.VMEM((n_row, 8, rhs), f32),
+            pltpu.VMEM(sums, f32),
         ),
-        in_specs=[in_hbm] * 2 + [smem] * 3 + [in_hbm] * 8,
+        in_specs=[in_hbm] * 13,
         out_specs=(vmem,) * 4,
         scratch_shapes=scratch,
         compiler_params=pltpu.CompilerParams(

time: 38.3 us -> 35 us (0.914)
  Pallas kernels: 35.6 us -> 32.2 us
    pallas_call x1, Pallas kernels: 34.9 us -> 31.6 us  [per_device(): pl.pallas_call(functools.partial(kernel, (n_row, n_col, unroll)), out_sha...]
where the time goes in v1:
time: 35 us; the launch traced here: 34.8 us
  Pallas kernels  32.2 us (92%)
  between operations  2.58 us (7%)
    pallas_call x1, Pallas kernels, per_device(): pl.pallas_call(functools.partial(kernel, (n_row, n_col, unroll)), out_sha...  31.6 us

profile of v1, /device:TPU:0, one launch (start us, length us, event | category | flops | bytes accessed | tf_op | source)
XLA Modules:
  0.0 34.8 jit_solution(6842978786105130217)
XLA Ops:
  2.6 31.6 %lsqr.1 = (f32[64,128]{1,0:T(8,128)S(1)}, f32[3,64,128]{2,1,0:T(8,128)S(1)}, f32[1,128]{1,0:T(1,128)S(1)}, f32[8,4,128]{2,1,0:T(4,128)S(1)}) custom-call(s32[1,1,16]{2,1,0:T(1,128)} %rows_hbm.1, s32[1,1,16]{2,1,0:T(1,128)} %cols_hbm.1, s32[1,1]{1,0:T(1,128)S(6)} %copy.16.count_hbm, s32[1,1]{1,0:T(1,128)S(6)} %copy.17.mid_rank_hbm, ...), custom_call_target="tpu_custom_call" | custom-call | tf_op jit(solution)/shard_map/lsqr/pallas_call | solution.py:466
  34.1 0.7 %finish.1 = (f32[64,128]{1,0:T(8,128)}, f32[3,64,128]{2,1,0:T(8,128)}, f32[2,128]{1,0:T(2,128)}) custom-call(f32[64,128]{1,0:T(8,128)S(1)} %get-tuple-element.7.u_ref, f32[3,64,128]{2,1,0:T(8,128)S(1)} %get-tuple-element.8.v_ref, f32[1,128]{1,0:T(1,128)S(1)} %get-tuple-element.9.beta_ref, f32[8,4,128]{2,1,0:T(4,128)S(1)} %get-tuple-element.10.squares_ref), custom_call_target="tpu_custom_call" | custom-call | tf_op jit(solution)/shard_map/finish/pallas_call | solution.py:496

commit v2 on v1

v2 whole, which is shorter than its diff:
```python
import functools

import jax
import jax.numpy as jnp
from jax import lax
from jax.experimental import pallas as pl
from jax.experimental.pallas import tpu as pltpu
from jax.sharding import PartitionSpec as P

tiny_add = 1e-06
MESH = pl.DeviceIdType.MESH
f32, bf16 = jnp.float32, jnp.bfloat16
WHOLE_LIMIT = 64


def fold(values):
    return (values * values).reshape(values.shape[0] // 8, 8, values.shape[1]).sum(axis=0)


def turn(values):
    return jnp.transpose(values.astype(f32), (1, 0))


def kernel(
    sizes,
    rows_hbm,
    cols_hbm,
    count_hbm,
    mid_rank_hbm,
    coarse_rank_hbm,
    u_hbm,
    v_hbm,
    alpha_hbm,
    near_hbm,
    mid_left_hbm,
    mid_right_hbm,
    coarse_left_hbm,
    coarse_right_hbm,
    u_out,
    v_out,
    beta_out,
    vsq_all,
    rows_smem,
    cols_smem,
    count_smem,
    mid_rank_smem,
    coarse_rank_smem,
    near,
    u_old,
    v_old,
    alpha_old,
    left,
    left_turned,
    right,
    slip,
    coarse_all,
    part_codes,
    weights,
    dense,
    dense_turned,
    fsend,
    frecv,
    ug,
    sq,
    bsend,
    brecv,
    vsq_col,
    near_sem,
    in_sem,
    slip_send,
    slip_recv,
    part_send,
    part_recv,
    coarse_send,
    coarse_recv,
    f_send,
    f_recv,
    u_send,
    u_recv,
    sq_send,
    sq_recv,
    b_send,
    b_recv,
    vc_send,
    vc_recv,
    vr_send,
    vr_recv,
):
    n_row, n_col = sizes
    me_r, me_c = lax.axis_index("row"), lax.axis_index("col")
    slots, _, clp, clq = near.shape
    pt, rhs = u_old.shape
    pd = v_old.shape[1]
    km, kc = mid_left_hbm.shape[0], coarse_left_hbm.shape[0]
    kt = km + kc
    row_span, col_span = left.shape[1], right.shape[2]
    row_groups, col_groups = row_span // clp, col_span // clq
    per_col = clq // pd
    spots = row_groups * col_groups
    bunch = 8 if spots % 8 == 0 else spots
    tile = 32

    def row_peer(step):
        return lax.rem(me_r + step, n_row)

    def far_first(me, count, step):
        upper = me >= count // 2
        own = jnp.where(upper, me, count - 1 - me)
        place = step - 1 + (step - 1 >= own).astype(jnp.int32)
        return jnp.where(upper, place, count - 1 - place)

    def col_peer(step):
        return far_first(me_c, n_col, step)

    loads = [
        pltpu.make_async_copy(src, dst, in_sem.at[place])
        for place, (src, dst) in enumerate(
            [
                (v_hbm, v_old),
                (coarse_right_hbm, coarse_all.at[me_r]),
                (rows_hbm, rows_smem),
                (cols_hbm, cols_smem),
                (count_hbm, count_smem),
                (mid_rank_hbm, mid_rank_smem),
                (coarse_rank_hbm, coarse_rank_smem),
                (mid_right_hbm, right.at[:, 0:km, :]),
                (mid_left_hbm, left.at[0:km, :]),
                (coarse_left_hbm, left.at[km:kt, :]),
                (u_hbm, u_old),
                (alpha_hbm, alpha_old),
            ]
        )
    ]
    loads[0].start()
    loads[1].start()

    barrier = pltpu.get_barrier_semaphore()
    for step in range(1, n_col):
        pl.semaphore_signal(barrier, device_id={"col": col_peer(step)}, device_id_type=MESH)
    for step in range(1, n_row):
        pl.semaphore_signal(barrier, device_id={"row": row_peer(step)}, device_id_type=MESH)
    pieces = near_sem.shape[0]
    share = slots // pieces
    near_loads = [
        pltpu.make_async_copy(
            near_hbm.at[pl.ds(piece * share, share)], near.at[pl.ds(piece * share, share)], near_sem.at[piece]
        )
        for piece in range(pieces)
    ]
    for load in near_loads:
        load.start()
    for load in loads[2:]:
        load.start()

    def exchange(axis, me, count, peer, source, target, send_sem, recv_sem, steps=None):
        copies = [
            pltpu.make_async_remote_copy(
                src_ref=source(peer(step)),
                dst_ref=target,
                send_sem=send_sem.at[step - 1],
                recv_sem=recv_sem.at[me],
                device_id={axis: peer(step)},
                device_id_type=MESH,
            )
            for step in range(1, count)
        ]
        for copy in copies:
            copy.start()
        incoming = [
            pltpu.make_async_remote_copy(
                src_ref=source(peer(step)),
                dst_ref=target,
                send_sem=send_sem.at[step - 1],
                recv_sem=recv_sem.at[peer(step)],
                device_id={axis: peer(step)},
                device_id_type=MESH,
            )
            for step in range(1, count)
        ]
        return copies, incoming

    def across_rows(source, target, send_sem, recv_sem):
        return exchange("row", me_r, n_row, row_peer, source, target, send_sem, recv_sem)

    def across_cols(source, target, send_sem, recv_sem):
        return exchange("col", me_c, n_col, col_peer, source, target, send_sem, recv_sem)

    def arrived(copies):
        for copy in copies[1]:
            copy.wait_recv()

    loads[0].wait()
    slip[me_r] = v_old[...].astype(bf16)
    loads[1].wait()
    own_codes = jnp.zeros((kc, rhs), f32)
    for k in range(3):
        own_codes = own_codes + jnp.dot(coarse_all[me_r, k], slip[me_r, k], preferred_element_type=f32)
    part_codes[me_r] = own_codes.astype(bf16)
    pl.semaphore_wait(barrier, n_row + n_col - 2)
    sent_slip = across_rows(lambda peer: slip.at[me_r], slip.at[me_r], slip_send, slip_recv)
    sent_part = across_rows(
        lambda peer: part_codes.at[me_r], part_codes.at[me_r], part_send, part_recv
    )
    for load in loads[2:]:
        load.wait()
    spot_of = lax.broadcasted_iota(jnp.int32, (spots, rhs), 0)
    for slot in range(slots):
        spot = cols_smem[0, 0, slot] * row_groups + rows_smem[0, 0, slot]
        spot = jnp.where(slot < count_smem[0, 0], spot, -1)
        weights[slot] = jnp.where(spot_of == spot, 1.0, 0.0).astype(f32)
    for group in range(row_groups):
        span = slice(group * clp, (group + 1) * clp)
        left_turned[span, :] = turn(left[:, span]).astype(bf16)
    for load in near_loads:
        load.wait()
    chunks = clp // tile

    def build(step, carry):
        chunk, k, first = step % chunks, (step // chunks) % 3, (step // (3 * chunks)) * bunch
        at = pl.multiple_of(chunk * tile, tile)
        sums = [jnp.zeros((tile, clq), f32)] * bunch
        for slot in range(slots):
            block = near[slot, k, pl.ds(at, tile), :].astype(f32)
            for place in range(bunch):
                sums[place] = sums[place] + block * weights[slot, pl.ds(first + place, 1), :]
        for place in range(bunch):
            spot = first + place
            group, wide = spot % row_groups, spot // row_groups
            dense[
                pl.ds(pl.multiple_of(group * clp + at, tile), tile),
                pl.ds(pl.multiple_of((wide * 3 + k) * clq, clq), clq),
            ] = sums[place].astype(bf16)
        return carry

    lax.fori_loop(0, spots // bunch * 3 * chunks, build, 0)
    arrived(sent_slip)
    sent_coarse = across_rows(
        lambda peer: coarse_all.at[me_r], coarse_all.at[me_r], coarse_send, coarse_recv
    )

    codes = jnp.zeros((km, rhs), f32)
    for k in range(3):
        codes = codes + jnp.dot(
            right[k, 0:km, :], slip[:, k].reshape(n_row * pd, rhs), preferred_element_type=f32
        )
    place = lax.broadcasted_iota(jnp.int32, (km, rhs), 0)
    codes = jnp.where(place < mid_rank_smem[0, 0], codes, 0.0).astype(bf16)
    arrived(sent_part)
    coarse_codes = jnp.zeros((kc, rhs), f32)
    for peer in range(n_row):
        coarse_codes = coarse_codes + part_codes[peer].astype(f32)
    place = lax.broadcasted_iota(jnp.int32, (kc, rhs), 0)
    coarse_codes = jnp.where(place < coarse_rank_smem[0], coarse_codes, 0.0).astype(bf16)
    codes = jnp.concatenate([codes, coarse_codes], axis=0)
    gathered = jnp.concatenate(
        [
            slip[wide * per_col : (wide + 1) * per_col, k].reshape(clq, rhs)
            for wide in range(col_groups)
            for k in range(3)
        ],
        axis=0,
    )
    wave = min(row_span, 512)
    for group in range(row_span // wave):
        span = slice(group * wave, (group + 1) * wave)
        value = jnp.dot(dense[span, :], gathered, preferred_element_type=f32)
        value = value + jnp.dot(left_turned[span, :], codes, preferred_element_type=f32)
        fsend[group * wave // pt : (group + 1) * wave // pt] = value.astype(bf16).reshape(
            wave // pt, pt, rhs
        )
    sent_f = across_cols(lambda peer: fsend.at[peer], frecv.at[me_c], f_send, f_recv)
    frecv[me_c] = fsend[me_c]

    arrived(sent_coarse)
    for peer in range(n_row):
        for k in range(3):
            right[k, km:kt, peer * pd : (peer + 1) * pd] = coarse_all[peer, k]
    place = lax.broadcasted_iota(jnp.int32, (kt, row_span), 0)
    limit = jnp.where(place < km, mid_rank_smem[0, 0], coarse_rank_smem[0] + km)
    left[...] = jnp.where(place < limit, left[...].astype(f32), 0.0).astype(bf16)

    def turn_over(step, carry):
        k, wide = step % 3, step // 3
        rank_turned = turn(right[k, :, pl.ds(pl.multiple_of(wide * clq, clq), clq)]).astype(bf16)
        for group in range(row_groups):
            span = slice(group * clp, (group + 1) * clp)
            value = jnp.dot(rank_turned, left[:, span], preferred_element_type=f32)
            value = value + turn(dense[span, pl.ds(pl.multiple_of(step * clq, clq), clq)])
            dense_turned[step, :, span] = value.astype(bf16)
        return carry

    lax.fori_loop(0, 3 * col_groups, turn_over, 0)

    arrived(sent_f)
    u_hat = -alpha_old[...] * u_old[...]
    for peer in range(n_col):
        u_hat = u_hat + frecv[peer].astype(f32)
    ug[me_c] = u_hat.astype(bf16)
    sent_u = across_cols(lambda peer: ug.at[me_c], ug.at[me_c], u_send, u_recv)
    u_old[...] = u_hat
    arrived(sent_u)

    gathered = ug[...].reshape(row_span, rhs)
    own_wide = me_r // per_col
    sent_b, incoming_b = [], []
    for turn_index in range(col_groups):
        wide = lax.rem(own_wide + 1 + turn_index, col_groups)
        for k in range(3):
            value = jnp.dot(dense_turned[wide * 3 + k], gathered, preferred_element_type=f32)
            value = value.astype(bf16).reshape(per_col, pd, rhs)
            for part in range(per_col):
                bsend[wide * per_col + part, k] = value[part]
        last = turn_index == col_groups - 1
        for part in range(per_col):
            if last:
                if part == 0:
                    continue
                peer = wide * per_col + lax.rem(lax.rem(me_r, per_col) + part, per_col)
            else:
                peer = wide * per_col + part
            slot = turn_index * per_col + part
            copy = pltpu.make_async_remote_copy(
                src_ref=bsend.at[peer],
                dst_ref=brecv.at[me_r],
                send_sem=b_send.at[slot],
                recv_sem=b_recv.at[me_r],
                device_id={"row": peer},
                device_id_type=MESH,
            )
            copy.start()
            sent_b.append(copy)
            incoming_b.append(
                pltpu.make_async_remote_copy(
                    src_ref=bsend.at[peer],
                    dst_ref=brecv.at[me_r],
                    send_sem=b_send.at[slot],
                    recv_sem=b_recv.at[peer],
                    device_id={"row": peer},
                    device_id_type=MESH,
                )
            )
        if turn_index == 0:
            sq[me_r] = fold(gathered.astype(f32))
            sent_sq = across_rows(lambda peer: sq.at[me_r], sq.at[me_r], sq_send, sq_recv)
    brecv[me_r] = bsend[me_r]
    sent_b = (sent_b, incoming_b)
    arrived(sent_sq)
    square_sum = jnp.zeros((8, rhs), f32)
    for peer in range(n_row):
        square_sum = square_sum + sq[peer]
    points = pt * n_row * n_col
    beta = jnp.sqrt(jnp.sum(square_sum, axis=0, keepdims=True) / points + tiny_add)
    beta_out[...] = beta
    u_out[...] = u_old[...] / beta
    arrived(sent_b)
    v_squares = jnp.zeros((8, rhs), f32)
    for k in range(3):
        total = jnp.zeros((pd, rhs), f32)
        for peer in range(n_row):
            total = total + brecv[peer, k].astype(f32)
        v_hat = total / beta - beta * v_old[k]
        v_out[k] = v_hat
        v_squares = v_squares + fold(v_hat)
    sent_v = []
    if n_row * n_col <= WHOLE_LIMIT:
        others = [(a, b) for b in range(n_col) for a in range(n_row)][1:]
        far = [(lax.rem(me_r + a, n_row), lax.rem(me_c + b, n_col)) for a, b in others]
        vsq_all[me_c, pl.ds(me_r, 1)] = jnp.sum(v_squares, axis=0, keepdims=True)

        def row_sum(place, row, col):
            return pltpu.make_async_remote_copy(
                src_ref=vsq_all.at[me_c, pl.ds(me_r, 1)],
                dst_ref=vsq_all.at[me_c, pl.ds(me_r, 1)],
                send_sem=vc_send.at[place],
                recv_sem=vc_recv.at[place],
                device_id=(row, col),
                device_id_type=MESH,
            )

        for place in reversed(range(len(far))):
            copy = row_sum(place, *far[place])
            copy.start()
            sent_v.append(copy)
        for copy in sent_v:
            copy.wait_recv()
    else:
        vsq_col[me_c] = v_squares
        sent_vc = across_cols(lambda peer: vsq_col.at[me_c], vsq_col.at[me_c], vc_send, vc_recv)
        arrived(sent_vc)
        v_squares = jnp.zeros((8, rhs), f32)
        for peer in range(n_col):
            v_squares = v_squares + vsq_col[peer]
        vsq_all[me_r] = v_squares
        sent_vr = across_rows(lambda peer: vsq_all.at[me_r], vsq_all.at[me_r], vr_send, vr_recv)
        arrived(sent_vr)
        sent_v = sent_vc[0] + sent_vr[0]
    for copies in (sent_slip, sent_part, sent_coarse, sent_f, sent_u, sent_sq, sent_b):
        for copy in copies[0]:
            copy.wait_send()
    for copy in sent_v:
        copy.wait_send()


def finish(unknowns, u_ref, v_ref, beta_ref, squares_ref, u_out, v_out, norms_out):
    total = jnp.zeros(squares_ref.shape[1:], f32)
    for peer in range(squares_ref.shape[0]):
        total = total + squares_ref[peer]
    alpha = jnp.sqrt(jnp.sum(total, axis=0, keepdims=True) / unknowns + tiny_add)
    norms_out[0:1, :] = beta_ref[...]
    norms_out[1:2, :] = alpha
    u_out[...] = u_ref[...]
    v_out[...] = v_ref[...] / alpha


def per_device(
    n_row,
    n_col,
    u_state,
    v_state,
    alpha_prev,
    near_blocks,
    near_rows,
    near_cols,
    near_count,
    mid_left,
    mid_right,
    mid_rank,
    coarse_left,
    coarse_right,
    coarse_rank,
):
    slots, clp, _, clq = near_blocks.shape[2:]
    pt, rhs = u_state.shape
    pd = v_state.shape[1]
    km, kc = mid_left.shape[1], coarse_left.shape[1]
    kt = km + kc
    row_span, col_span = mid_left.shape[2], mid_right.shape[3]
    row_groups, col_groups = row_span // clp, col_span // clq
    in_hbm = pl.BlockSpec(memory_space=pltpu.HBM)
    vmem = pl.BlockSpec(memory_space=pltpu.VMEM)
    dma = pltpu.SemaphoreType.DMA
    row_sem, col_sem = dma((n_row,)), dma((n_col,))
    whole = n_row * n_col <= WHOLE_LIMIT
    last_sem = dma((n_row * n_col,)) if whole else col_sem
    sums = (n_col, n_row, rhs) if whole else (n_row, 8, rhs)
    scratch = [
        pltpu.SMEM(near_rows.shape, jnp.int32),
        pltpu.SMEM(near_cols.shape, jnp.int32),
        pltpu.SMEM(near_count.shape, jnp.int32),
        pltpu.SMEM(mid_rank.shape, jnp.int32),
        pltpu.SMEM(coarse_rank.shape, jnp.int32),
        pltpu.VMEM((slots, 3, clp, clq), bf16),
        pltpu.VMEM((pt, rhs), f32),
        pltpu.VMEM((3, pd, rhs), f32),
        pltpu.VMEM((1, rhs), f32),
        pltpu.VMEM((kt, row_span), bf16),
        pltpu.VMEM((row_span, kt), bf16),
        pltpu.VMEM((3, kt, col_span), bf16),
        pltpu.VMEM((n_row, 3, pd, rhs), bf16),
        pltpu.VMEM((n_row, 3, kc, pd), bf16),
        pltpu.VMEM((n_row, kc, rhs), bf16),
        pltpu.VMEM((slots, row_groups * col_groups, rhs), f32),
        pltpu.VMEM((row_span, 3 * col_span), bf16),
        pltpu.VMEM((3 * col_groups, clq, row_span), bf16),
        pltpu.VMEM((n_col, pt, rhs), bf16),
        pltpu.VMEM((n_col, pt, rhs), bf16),
        pltpu.VMEM((n_col, pt, rhs), bf16),
        pltpu.VMEM((n_row, 8, rhs), f32),
        pltpu.VMEM((n_row, 3, pd, rhs), bf16),
        pltpu.VMEM((n_row, 3, pd, rhs), bf16),
        pltpu.VMEM((n_col, 8, rhs), f32),
        dma((4 if slots % 4 == 0 else 1,)),
        dma((12,)),
        row_sem,
        row_sem,
        row_sem,
        row_sem,
        row_sem,
        row_sem,
        col_sem,
        col_sem,
        col_sem,
        col_sem,
        row_sem,
        row_sem,
        row_sem,
        row_sem,
        last_sem,
        last_sem,
        row_sem,
        row_sem,
    ]
    held = pl.pallas_call(
        functools.partial(kernel, (n_row, n_col)),
        out_shape=(
            pltpu.VMEM((pt, rhs), f32),
            pltpu.VMEM((3, pd, rhs), f32),
            pltpu.VMEM((1, rhs), f32),
            pltpu.VMEM(sums, f32),
        ),
        in_specs=[in_hbm] * 13,
        out_specs=(vmem,) * 4,
        scratch_shapes=scratch,
        compiler_params=pltpu.CompilerParams(
            collective_id=0, has_side_effects=True, vmem_limit_bytes=60 * 1024 * 1024
        ),
        name="lsqr",
    )(
        near_rows,
        near_cols,
        near_count,
        mid_rank,
        coarse_rank,
        u_state,
        v_state,
        alpha_prev.reshape(1, rhs),
        jnp.transpose(near_blocks[0, 0], (0, 2, 1, 3)),
        mid_left[0],
        jnp.transpose(mid_right[0], (1, 0, 2)),
        coarse_left[0],
        jnp.transpose(coarse_right, (1, 0, 2)),
    )
    return pl.pallas_call(
        functools.partial(finish, 3 * pd * n_row * n_col),
        out_shape=(
            jax.ShapeDtypeStruct((pt, rhs), f32),
            jax.ShapeDtypeStruct((3, pd, rhs), f32),
            jax.ShapeDtypeStruct((2, rhs), f32),
        ),
        in_specs=[vmem] * 4,
        out_specs=(vmem,) * 3,
        name="finish",
    )(*[pltpu.with_memory_space_constraint(value, pltpu.VMEM) for value in held])


def solution(mesh):
    placed = (
        P(("row", "col"), None),
        P(None, ("col", "row"), None),
        P(),
        P("row", "col", None, None, None, None),
        P("row", "col", None),
        P("row", "col", None),
        P("row", "col"),
        P("col", None, "row"),
        P("row", None, None, "col"),
        P("row", "col"),
        P("col", None, "row"),
        P(None, None, ("col", "row")),
        P("col"),
    )
    return jax.shard_map(
        functools.partial(per_device, mesh.shape["row"], mesh.shape["col"]),
        mesh=mesh,
        in_specs=placed,
        out_specs=(P(("row", "col"), None), P(None, ("col", "row"), None), P()),
        check_vma=False,
    )
```

time: 35 us -> 33.3 us (0.951)
  Pallas kernels: 32.2 us -> 30.5 us
    pallas_call x1, Pallas kernels: 31.6 us -> 29.9 us  [per_device(): pl.pallas_call(functools.partial(kernel, (n_row, n_col)), out_shape=(pltp...]
where the time goes in v2:
time: 33.3 us; the launch traced here: 33.1 us
  Pallas kernels  30.5 us (92%)
  between operations  2.58 us (8%)
    pallas_call x1, Pallas kernels, per_device(): pl.pallas_call(functools.partial(kernel, (n_row, n_col)), out_shape=(pltp...  29.9 us
    pallas_call x1, Pallas kernels, per_device(): pl.pallas_call(functools.partial(finish, 3 * pd * n_row * n_col), out_sha...  0.68 us

profile of v2, /device:TPU:0, one launch (start us, length us, event | category | flops | bytes accessed | tf_op | source)
XLA Modules:
  0.0 33.1 jit_solution(10704545974996517756)
XLA Ops:
  2.6 29.9 %lsqr.1 = (f32[64,128]{1,0:T(8,128)S(1)}, f32[3,64,128]{2,1,0:T(8,128)S(1)}, f32[1,128]{1,0:T(1,128)S(1)}, f32[8,4,128]{2,1,0:T(4,128)S(1)}) custom-call(s32[1,1,16]{2,1,0:T(1,128)} %rows_hbm.1, s32[1,1,16]{2,1,0:T(1,128)} %cols_hbm.1, s32[1,1]{1,0:T(1,128)S(6)} %copy.16.count_hbm, s32[1,1]{1,0:T(1,128)S(6)} %copy.17.mid_rank_hbm, ...), custom_call_target="tpu_custom_call" | custom-call | tf_op jit(solution)/shard_map/lsqr/pallas_call | solution.py:493
  32.4 0.7 %finish.1 = (f32[64,128]{1,0:T(8,128)}, f32[3,64,128]{2,1,0:T(8,128)}, f32[2,128]{1,0:T(2,128)}) custom-call(f32[64,128]{1,0:T(8,128)S(1)} %get-tuple-element.7.u_ref, f32[3,64,128]{2,1,0:T(8,128)S(1)} %get-tuple-element.8.v_ref, f32[1,128]{1,0:T(1,128)S(1)} %get-tuple-element.9.beta_ref, f32[8,4,128]{2,1,0:T(4,128)S(1)} %get-tuple-element.10.squares_ref), custom_call_target="tpu_custom_call" | custom-call | tf_op jit(solution)/shard_map/finish/pallas_call | solution.py:523

commit v3 on v2

--- a/solution.py
+++ b/solution.py
@@ -11,6 +11,7 @@
 MESH = pl.DeviceIdType.MESH
 f32, bf16 = jnp.float32, jnp.bfloat16
 WHOLE_LIMIT = 64
+COARSE, SLIP, SUMS, LEFT, SQUARES, BACK, ALL, COLS, PARTS = range(9)
 
 
 def fold(values):
@@ -67,24 +68,8 @@
     vsq_col,
     near_sem,
     in_sem,
-    slip_send,
-    slip_recv,
-    part_send,
-    part_recv,
-    coarse_send,
-    coarse_recv,
-    f_send,
-    f_recv,
-    u_send,
-    u_recv,
-    sq_send,
-    sq_recv,
-    b_send,
-    b_recv,
-    vc_send,
-    vc_recv,
-    vr_send,
-    vr_recv,
+    send_sem,
+    recv_sem,
 ):
     n_row, n_col = sizes
     me_r, me_c = lax.axis_index("row"), lax.axis_index("col")
@@ -139,11 +124,11 @@
         pl.semaphore_signal(barrier, device_id={"col": col_peer(step)}, device_id_type=MESH)
     for step in range(1, n_row):
         pl.semaphore_signal(barrier, device_id={"row": row_peer(step)}, device_id_type=MESH)
-    pieces = near_sem.shape[0]
+    pieces = 4 if slots % 4 == 0 else 1
     share = slots // pieces
     near_loads = [
         pltpu.make_async_copy(
-            near_hbm.at[pl.ds(piece * share, share)], near.at[pl.ds(piece * share, share)], near_sem.at[piece]
+            near_hbm.at[pl.ds(piece * share, share)], near.at[pl.ds(piece * share, share)], near_sem
         )
         for piece in range(pieces)
     ]
@@ -152,42 +137,27 @@
     for load in loads[2:]:
         load.start()
 
-    def exchange(axis, me, count, peer, source, target, send_sem, recv_sem, steps=None):
-        copies = [
-            pltpu.make_async_remote_copy(
-                src_ref=source(peer(step)),
-                dst_ref=target,
-                send_sem=send_sem.at[step - 1],
-                recv_sem=recv_sem.at[me],
-                device_id={axis: peer(step)},
-                device_id_type=MESH,
-            )
-            for step in range(1, count)
-        ]
-        for copy in copies:
-            copy.start()
-        incoming = [
-            pltpu.make_async_remote_copy(
-                src_ref=source(peer(step)),
-                dst_ref=target,
-                send_sem=send_sem.at[step - 1],
-                recv_sem=recv_sem.at[peer(step)],
-                device_id={axis: peer(step)},
-                device_id_type=MESH,
-            )
-            for step in range(1, count)
-        ]
-        return copies, incoming
-
-    def across_rows(source, target, send_sem, recv_sem):
-        return exchange("row", me_r, n_row, row_peer, source, target, send_sem, recv_sem)
-
-    def across_cols(source, target, send_sem, recv_sem):
-        return exchange("col", me_c, n_col, col_peer, source, target, send_sem, recv_sem)
-
-    def arrived(copies):
-        for copy in copies[1]:
-            copy.wait_recv()
+    def post(place, device, source, target):
+        copy = pltpu.make_async_remote_copy(
+            src_ref=source,
+            dst_ref=target,
+            send_sem=send_sem.at[place],
+            recv_sem=recv_sem.at[place],
+            device_id=device,
+            device_id_type=MESH,
+        )
+        return copy
+
+    def across_rows(place, source, target):
+        for step in range(1, n_row):
+            post(place, {"row": row_peer(step)}, source(row_peer(step)), target).start()
+
+    def across_cols(place, source, target):
+        for step in range(1, n_col):
+            post(place, {"col": col_peer(step)}, source(col_peer(step)), target).start()
+
+    def every(place, buffer, count):
+        return post(place, {"row": row_peer(1)}, buffer.at[pl.ds(0, count - 1)], buffer.at[pl.ds(0, count - 1)])
 
     loads[0].wait()
     slip[me_r] = v_old[...].astype(bf16)
@@ -197,10 +167,8 @@
         own_codes = own_codes + jnp.dot(coarse_all[me_r, k], slip[me_r, k], preferred_element_type=f32)
     part_codes[me_r] = own_codes.astype(bf16)
     pl.semaphore_wait(barrier, n_row + n_col - 2)
-    sent_slip = across_rows(lambda peer: slip.at[me_r], slip.at[me_r], slip_send, slip_recv)
-    sent_part = across_rows(
-        lambda peer: part_codes.at[me_r], part_codes.at[me_r], part_send, part_recv
-    )
+    across_rows(PARTS, lambda peer: part_codes.at[me_r], part_codes.at[me_r])
+    across_rows(SLIP, lambda peer: slip.at[me_r], slip.at[me_r])
     for load in loads[2:]:
         load.wait()
     spot_of = lax.broadcasted_iota(jnp.int32, (spots, rhs), 0)
@@ -211,8 +179,7 @@
     for group in range(row_groups):
         span = slice(group * clp, (group + 1) * clp)
         left_turned[span, :] = turn(left[:, span]).astype(bf16)
-    for load in near_loads:
-        load.wait()
+    pltpu.make_async_copy(near_hbm, near, near_sem).wait()
     chunks = clp // tile
 
     def build(step, carry):
@@ -233,11 +200,14 @@
         return carry
 
     lax.fori_loop(0, spots // bunch * 3 * chunks, build, 0)
-    arrived(sent_slip)
-    sent_coarse = across_rows(
-        lambda peer: coarse_all.at[me_r], coarse_all.at[me_r], coarse_send, coarse_recv
-    )
-
+    across_rows(COARSE, lambda peer: coarse_all.at[me_r], coarse_all.at[me_r])
+    every(PARTS, part_codes, n_row).wait_recv()
+    coarse_codes = jnp.zeros((kc, rhs), f32)
+    for peer in range(n_row):
+        coarse_codes = coarse_codes + part_codes[peer].astype(f32)
+    place = lax.broadcasted_iota(jnp.int32, (kc, rhs), 0)
+    coarse_codes = jnp.where(place < coarse_rank_smem[0], coarse_codes, 0.0).astype(bf16)
+    every(SLIP, slip, n_row).wait_recv()
     codes = jnp.zeros((km, rhs), f32)
     for k in range(3):
         codes = codes + jnp.dot(
@@ -245,12 +215,6 @@
         )
     place = lax.broadcasted_iota(jnp.int32, (km, rhs), 0)
     codes = jnp.where(place < mid_rank_smem[0, 0], codes, 0.0).astype(bf16)
-    arrived(sent_part)
-    coarse_codes = jnp.zeros((kc, rhs), f32)
-    for peer in range(n_row):
-        coarse_codes = coarse_codes + part_codes[peer].astype(f32)
-    place = lax.broadcasted_iota(jnp.int32, (kc, rhs), 0)
-    coarse_codes = jnp.where(place < coarse_rank_smem[0], coarse_codes, 0.0).astype(bf16)
     codes = jnp.concatenate([codes, coarse_codes], axis=0)
     gathered = jnp.concatenate(
         [
@@ -268,10 +232,10 @@
         fsend[group * wave // pt : (group + 1) * wave // pt] = value.astype(bf16).reshape(
             wave // pt, pt, rhs
         )
-    sent_f = across_cols(lambda peer: fsend.at[peer], frecv.at[me_c], f_send, f_recv)
+    across_cols(SUMS, lambda peer: fsend.at[peer], frecv.at[me_c])
     frecv[me_c] = fsend[me_c]
 
-    arrived(sent_coarse)
+    every(COARSE, coarse_all, n_row).wait_recv()
     for peer in range(n_row):
         for k in range(3):
             right[k, km:kt, peer * pd : (peer + 1) * pd] = coarse_all[peer, k]
@@ -291,18 +255,17 @@
 
     lax.fori_loop(0, 3 * col_groups, turn_over, 0)
 
-    arrived(sent_f)
+    every(SUMS, frecv, n_col).wait_recv()
     u_hat = -alpha_old[...] * u_old[...]
     for peer in range(n_col):
         u_hat = u_hat + frecv[peer].astype(f32)
     ug[me_c] = u_hat.astype(bf16)
-    sent_u = across_cols(lambda peer: ug.at[me_c], ug.at[me_c], u_send, u_recv)
+    across_cols(LEFT, lambda peer: ug.at[me_c], ug.at[me_c])
     u_old[...] = u_hat
-    arrived(sent_u)
+    every(LEFT, ug, n_col).wait_recv()
 
     gathered = ug[...].reshape(row_span, rhs)
     own_wide = me_r // per_col
-    sent_b, incoming_b = [], []
     for turn_index in range(col_groups):
         wide = lax.rem(own_wide + 1 + turn_index, col_groups)
         for k in range(3):
@@ -318,33 +281,12 @@
                 peer = wide * per_col + lax.rem(lax.rem(me_r, per_col) + part, per_col)
             else:
                 peer = wide * per_col + part
-            slot = turn_index * per_col + part
-            copy = pltpu.make_async_remote_copy(
-                src_ref=bsend.at[peer],
-                dst_ref=brecv.at[me_r],
-                send_sem=b_send.at[slot],
-                recv_sem=b_recv.at[me_r],
-                device_id={"row": peer},
-                device_id_type=MESH,
-            )
-            copy.start()
-            sent_b.append(copy)
-            incoming_b.append(
-                pltpu.make_async_remote_copy(
-                    src_ref=bsend.at[peer],
-                    dst_ref=brecv.at[me_r],
-                    send_sem=b_send.at[slot],
-                    recv_sem=b_recv.at[peer],
-                    device_id={"row": peer},
-                    device_id_type=MESH,
-                )
-            )
+            post(BACK, {"row": peer}, bsend.at[peer], brecv.at[me_r]).start()
         if turn_index == 0:
             sq[me_r] = fold(gathered.astype(f32))
-            sent_sq = across_rows(lambda peer: sq.at[me_r], sq.at[me_r], sq_send, sq_recv)
+            across_rows(SQUARES, lambda peer: sq.at[me_r], sq.at[me_r])
     brecv[me_r] = bsend[me_r]
-    sent_b = (sent_b, incoming_b)
-    arrived(sent_sq)
+    every(SQUARES, sq, n_row).wait_recv()
     square_sum = jnp.zeros((8, rhs), f32)
     for peer in range(n_row):
         square_sum = square_sum + sq[peer]
@@ -352,7 +294,7 @@
     beta = jnp.sqrt(jnp.sum(square_sum, axis=0, keepdims=True) / points + tiny_add)
     beta_out[...] = beta
     u_out[...] = u_old[...] / beta
-    arrived(sent_b)
+    every(BACK, brecv, n_row).wait_recv()
     v_squares = jnp.zeros((8, rhs), f32)
     for k in range(3):
         total = jnp.zeros((pd, rhs), f32)
@@ -361,44 +303,35 @@
         v_hat = total / beta - beta * v_old[k]
         v_out[k] = v_hat
         v_squares = v_squares + fold(v_hat)
-    sent_v = []
     if n_row * n_col <= WHOLE_LIMIT:
-        others = [(a, b) for b in range(n_col) for a in range(n_row)][1:]
-        far = [(lax.rem(me_r + a, n_row), lax.rem(me_c + b, n_col)) for a, b in others]
-        vsq_all[me_c, pl.ds(me_r, 1)] = jnp.sum(v_squares, axis=0, keepdims=True)
-
-        def row_sum(place, row, col):
-            return pltpu.make_async_remote_copy(
-                src_ref=vsq_all.at[me_c, pl.ds(me_r, 1)],
-                dst_ref=vsq_all.at[me_c, pl.ds(me_r, 1)],
-                send_sem=vc_send.at[place],
-                recv_sem=vc_recv.at[place],
-                device_id=(row, col),
-                device_id_type=MESH,
-            )
-
-        for place in reversed(range(len(far))):
-            copy = row_sum(place, *far[place])
-            copy.start()
-            sent_v.append(copy)
-        for copy in sent_v:
-            copy.wait_recv()
+        others = [(a, b) for b in reversed(range(n_col)) for a in reversed(range(n_row))][:-1]
+        own = vsq_all.at[me_c * n_row + me_r]
+        vsq_all[me_c * n_row + me_r] = jnp.sum(v_squares, axis=0, keepdims=True)
+        for a, b in others:
+            post(ALL, (lax.rem(me_r + a, n_row), lax.rem(me_c + b, n_col)), own, own).start()
+        every(ALL, vsq_all, n_row * n_col).wait_recv()
     else:
         vsq_col[me_c] = v_squares
-        sent_vc = across_cols(lambda peer: vsq_col.at[me_c], vsq_col.at[me_c], vc_send, vc_recv)
-        arrived(sent_vc)
+        across_cols(COLS, lambda peer: vsq_col.at[me_c], vsq_col.at[me_c])
+        every(COLS, vsq_col, n_col).wait_recv()
         v_squares = jnp.zeros((8, rhs), f32)
         for peer in range(n_col):
             v_squares = v_squares + vsq_col[peer]
         vsq_all[me_r] = v_squares
-        sent_vr = across_rows(lambda peer: vsq_all.at[me_r], vsq_all.at[me_r], vr_send, vr_recv)
-        arrived(sent_vr)
-        sent_v = sent_vc[0] + sent_vr[0]
-    for copies in (sent_slip, sent_part, sent_coarse, sent_f, sent_u, sent_sq, sent_b):
-        for copy in copies[0]:
-            copy.wait_send()
-    for copy in sent_v:
-        copy.wait_send()
+        across_rows(ALL, lambda peer: vsq_all.at[me_r], vsq_all.at[me_r])
+        every(ALL, vsq_all, n_row).wait_recv()
+        every(COLS, vsq_col, n_col).wait_send()
+    for place, buffer in (
+        (PARTS, part_codes),
+        (COARSE, coarse_all),
+        (SLIP, slip),
+        (SUMS, fsend),
+        (LEFT, ug),
+        (SQUARES, sq),
+        (BACK, bsend),
+        (ALL, vsq_all),
+    ):
+        every(place, buffer, buffer.shape[0]).wait_send()
 
 
 def finish(unknowns, u_ref, v_ref, beta_ref, squares_ref, u_out, v_out, norms_out):
@@ -439,10 +372,8 @@
     in_hbm = pl.BlockSpec(memory_space=pltpu.HBM)
     vmem = pl.BlockSpec(memory_space=pltpu.VMEM)
     dma = pltpu.SemaphoreType.DMA
-    row_sem, col_sem = dma((n_row,)), dma((n_col,))
     whole = n_row * n_col <= WHOLE_LIMIT
-    last_sem = dma((n_row * n_col,)) if whole else col_sem
-    sums = (n_col, n_row, rhs) if whole else (n_row, 8, rhs)
+    sums = (n_row * n_col, 1, rhs) if whole else (n_row, 8, rhs)
     scratch = [
         pltpu.SMEM(near_rows.shape, jnp.int32),
         pltpu.SMEM(near_cols.shape, jnp.int32),
@@ -469,26 +400,10 @@
         pltpu.VMEM((n_row, 3, pd, rhs), bf16),
         pltpu.VMEM((n_row, 3, pd, rhs), bf16),
         pltpu.VMEM((n_col, 8, rhs), f32),
-        dma((4 if slots % 4 == 0 else 1,)),
+        dma,
         dma((12,)),
-        row_sem,
-        row_sem,
-        row_sem,
-        row_sem,
-        row_sem,
-        row_sem,
-        col_sem,
-        col_sem,
-        col_sem,
-        col_sem,
-        row_sem,
-        row_sem,
-        row_sem,
-        row_sem,
-        last_sem,
-        last_sem,
-        row_sem,
-        row_sem,
+        dma((9,)),
+        dma((9,)),
     ]
     held = pl.pallas_call(
         functools.partial(kernel, (n_row, n_col)),

time: 33.3 us -> 32.3 us (0.970)
  Pallas kernels: 30.5 us -> 29.6 us
    pallas_call x1, Pallas kernels: 29.9 us -> 28.9 us  [per_device(): pl.pallas_call(functools.partial(kernel, (n_row, n_col)), out_shape=(pltp...]
where the time goes in v3:
time: 32.3 us; the launch traced here: 32.2 us
  Pallas kernels  29.6 us (92%)
  between operations  2.58 us (8%)
    pallas_call x1, Pallas kernels, per_device(): pl.pallas_call(functools.partial(kernel, (n_row, n_col)), out_shape=(pltp...  28.9 us
    pallas_call x1, Pallas kernels, per_device(): pl.pallas_call(functools.partial(finish, 3 * pd * n_row * n_col), out_sha...  0.7 us

profile of v3, /device:TPU:0, one launch (start us, length us, event | category | flops | bytes accessed | tf_op | source)
XLA Modules:
  0.0 32.2 jit_solution(17779462066564486210)
XLA Ops:
  2.6 28.9 %lsqr.1 = (f32[64,128]{1,0:T(8,128)S(1)}, f32[3,64,128]{2,1,0:T(8,128)S(1)}, f32[1,128]{1,0:T(1,128)S(1)}, f32[32,1,128]{2,1,0:T(1,128)S(1)}) custom-call(s32[1,1,16]{2,1,0:T(1,128)} %rows_hbm.1, s32[1,1,16]{2,1,0:T(1,128)} %cols_hbm.1, s32[1,1]{1,0:T(1,128)S(6)} %copy.16.count_hbm, s32[1,1]{1,0:T(1,128)S(6)} %copy.17.mid_rank_hbm, ...), custom_call_target="tpu_custom_call" | custom-call | tf_op jit(solution)/shard_map/lsqr/pallas_call | solution.py:408
  31.5 0.7 %finish.1 = (f32[64,128]{1,0:T(8,128)}, f32[3,64,128]{2,1,0:T(8,128)}, f32[2,128]{1,0:T(2,128)}) custom-call(f32[64,128]{1,0:T(8,128)S(1)} %get-tuple-element.7.u_ref, f32[3,64,128]{2,1,0:T(8,128)S(1)} %get-tuple-element.8.v_ref, f32[1,128]{1,0:T(1,128)S(1)} %get-tuple-element.9.beta_ref, f32[32,1,128]{2,1,0:T(1,128)S(1)} %get-tuple-element.10.squares_ref), custom_call_target="tpu_custom_call" | custom-call | tf_op jit(solution)/shard_map/finish/pallas_call | solution.py:438

commit v4 on v3

--- a/solution.py
+++ b/solution.py
@@ -55,6 +55,8 @@
     right,
     slip,
     coarse_all,
+    coarse_wide,
+    begun,
     part_codes,
     weights,
     dense,
@@ -85,17 +87,28 @@
     bunch = 8 if spots % 8 == 0 else spots
     tile = 32
 
-    def row_peer(step):
-        return lax.rem(me_r + step, n_row)
-
-    def far_first(me, count, step):
-        upper = me >= count // 2
-        own = jnp.where(upper, me, count - 1 - me)
-        place = step - 1 + (step - 1 >= own).astype(jnp.int32)
-        return jnp.where(upper, place, count - 1 - place)
-
-    def col_peer(step):
-        return far_first(me_c, n_col, step)
+    def flipped(me, mask):
+        place, bit = me, 1
+        while bit <= mask:
+            if mask & bit:
+                place = place + (1 - 2 * ((me // bit) % 2)) * bit
+            bit *= 2
+        return place
+
+    if n_col & (n_col - 1):
+        col_peers = [lax.rem(me_c + step, n_col) for step in range(1, n_col)]
+    else:
+        masks = list(range(n_col - 1, 0, -2)) + list(range(n_col - 2, 0, -2))
+        col_peers = [flipped(me_c, mask) for mask in masks]
+    if n_row % 2:
+        row_peers = [lax.rem(me_r + step, n_row) for step in range(1, n_row)]
+    else:
+        own_chip, core = me_r // 2, lax.rem(me_r, 2)
+        row_peers = []
+        for step in range(1, n_row // 2):
+            chip = lax.rem(own_chip + step, n_row // 2)
+            row_peers += [chip * 2 + 1 - core, chip * 2 + core]
+        row_peers += [own_chip * 2 + 1 - core]
 
     loads = [
         pltpu.make_async_copy(src, dst, in_sem.at[place])
@@ -108,7 +121,7 @@
                 (count_hbm, count_smem),
                 (mid_rank_hbm, mid_rank_smem),
                 (coarse_rank_hbm, coarse_rank_smem),
-                (mid_right_hbm, right.at[:, 0:km, :]),
+                (mid_right_hbm, right),
                 (mid_left_hbm, left.at[0:km, :]),
                 (coarse_left_hbm, left.at[km:kt, :]),
                 (u_hbm, u_old),
@@ -120,10 +133,10 @@
     loads[1].start()
 
     barrier = pltpu.get_barrier_semaphore()
-    for step in range(1, n_col):
-        pl.semaphore_signal(barrier, device_id={"col": col_peer(step)}, device_id_type=MESH)
-    for step in range(1, n_row):
-        pl.semaphore_signal(barrier, device_id={"row": row_peer(step)}, device_id_type=MESH)
+    for peer in col_peers:
+        pl.semaphore_signal(barrier, device_id={"col": peer}, device_id_type=MESH)
+    for peer in row_peers:
+        pl.semaphore_signal(barrier, device_id={"row": peer}, device_id_type=MESH)
     pieces = 4 if slots % 4 == 0 else 1
     share = slots // pieces
     near_loads = [
@@ -149,15 +162,15 @@
         return copy
 
     def across_rows(place, source, target):
-        for step in range(1, n_row):
-            post(place, {"row": row_peer(step)}, source(row_peer(step)), target).start()
+        for peer in row_peers:
+            post(place, {"row": peer}, source(peer), target).start()
 
     def across_cols(place, source, target):
-        for step in range(1, n_col):
-            post(place, {"col": col_peer(step)}, source(col_peer(step)), target).start()
+        for peer in col_peers:
+            post(place, {"col": peer}, source(peer), target).start()
 
     def every(place, buffer, count):
-        return post(place, {"row": row_peer(1)}, buffer.at[pl.ds(0, count - 1)], buffer.at[pl.ds(0, count - 1)])
+        return post(place, {"row": row_peers[0]}, buffer.at[pl.ds(0, count - 1)], buffer.at[pl.ds(0, count - 1)])
 
     loads[0].wait()
     slip[me_r] = v_old[...].astype(bf16)
@@ -171,6 +184,9 @@
     across_rows(SLIP, lambda peer: slip.at[me_r], slip.at[me_r])
     for load in loads[2:]:
         load.wait()
+    place = lax.broadcasted_iota(jnp.int32, (kt, row_span), 0)
+    limit = jnp.where(place < km, mid_rank_smem[0, 0], coarse_rank_smem[0] + km)
+    left[...] = jnp.where(place < limit, left[...].astype(f32), 0.0).astype(bf16)
     spot_of = lax.broadcasted_iota(jnp.int32, (spots, rhs), 0)
     for slot in range(slots):
         spot = cols_smem[0, 0, slot] * row_groups + rows_smem[0, 0, slot]
@@ -182,21 +198,33 @@
     pltpu.make_async_copy(near_hbm, near, near_sem).wait()
     chunks = clp // tile
 
+    sets = max(1, bunch // row_groups)
+    each = bunch // sets
+
     def build(step, carry):
-        chunk, k, first = step % chunks, (step // chunks) % 3, (step // (3 * chunks)) * bunch
+        chunk, k = step % chunks, (step // chunks) % 3
+        first = step // (3 * chunks) * bunch if spots > bunch else 0
         at = pl.multiple_of(chunk * tile, tile)
         sums = [jnp.zeros((tile, clq), f32)] * bunch
         for slot in range(slots):
             block = near[slot, k, pl.ds(at, tile), :].astype(f32)
             for place in range(bunch):
                 sums[place] = sums[place] + block * weights[slot, pl.ds(first + place, 1), :]
-        for place in range(bunch):
-            spot = first + place
-            group, wide = spot % row_groups, spot // row_groups
-            dense[
-                pl.ds(pl.multiple_of(group * clp + at, tile), tile),
-                pl.ds(pl.multiple_of((wide * 3 + k) * clq, clq), clq),
-            ] = sums[place].astype(bf16)
+        for part in range(sets):
+            places = range(part * each, (part + 1) * each)
+            wide = (first + part * each) // row_groups
+            groups = [(first + place) % row_groups for place in places]
+            ranks = jnp.concatenate(
+                [left_turned[pl.ds(pl.multiple_of(group * clp + at, tile), tile), 0:km] for group in groups], axis=0
+            )
+            low = jnp.dot(
+                ranks, right[k, :, pl.ds(pl.multiple_of(wide * clq, clq), clq)], preferred_element_type=f32
+            )
+            for number, (place, group) in enumerate(zip(places, groups)):
+                dense[
+                    pl.ds(pl.multiple_of(group * clp + at, tile), tile),
+                    pl.ds(pl.multiple_of((wide * 3 + k) * clq, clq), clq),
+                ] = (sums[place] + low[number * tile : (number + 1) * tile]).astype(bf16)
         return carry
 
     lax.fori_loop(0, spots // bunch * 3 * chunks, build, 0)
@@ -205,17 +233,12 @@
     coarse_codes = jnp.zeros((kc, rhs), f32)
     for peer in range(n_row):
         coarse_codes = coarse_codes + part_codes[peer].astype(f32)
-    place = lax.broadcasted_iota(jnp.int32, (kc, rhs), 0)
-    coarse_codes = jnp.where(place < coarse_rank_smem[0], coarse_codes, 0.0).astype(bf16)
+    coarse_codes = coarse_codes.astype(bf16)
+    wave = min(row_span, 512)
+    for group in range(row_span // wave):
+        span = slice(group * wave, (group + 1) * wave)
+        begun[span, :] = jnp.dot(left_turned[span, km:kt], coarse_codes, preferred_element_type=f32)
     every(SLIP, slip, n_row).wait_recv()
-    codes = jnp.zeros((km, rhs), f32)
-    for k in range(3):
-        codes = codes + jnp.dot(
-            right[k, 0:km, :], slip[:, k].reshape(n_row * pd, rhs), preferred_element_type=f32
-        )
-    place = lax.broadcasted_iota(jnp.int32, (km, rhs), 0)
-    codes = jnp.where(place < mid_rank_smem[0, 0], codes, 0.0).astype(bf16)
-    codes = jnp.concatenate([codes, coarse_codes], axis=0)
     gathered = jnp.concatenate(
         [
             slip[wide * per_col : (wide + 1) * per_col, k].reshape(clq, rhs)
@@ -224,11 +247,9 @@
         ],
         axis=0,
     )
-    wave = min(row_span, 512)
     for group in range(row_span // wave):
         span = slice(group * wave, (group + 1) * wave)
-        value = jnp.dot(dense[span, :], gathered, preferred_element_type=f32)
-        value = value + jnp.dot(left_turned[span, :], codes, preferred_element_type=f32)
+        value = begun[span, :] + jnp.dot(dense[span, :], gathered, preferred_element_type=f32)
         fsend[group * wave // pt : (group + 1) * wave // pt] = value.astype(bf16).reshape(
             wave // pt, pt, rhs
         )
@@ -238,17 +259,14 @@
     every(COARSE, coarse_all, n_row).wait_recv()
     for peer in range(n_row):
         for k in range(3):
-            right[k, km:kt, peer * pd : (peer + 1) * pd] = coarse_all[peer, k]
-    place = lax.broadcasted_iota(jnp.int32, (kt, row_span), 0)
-    limit = jnp.where(place < km, mid_rank_smem[0, 0], coarse_rank_smem[0] + km)
-    left[...] = jnp.where(place < limit, left[...].astype(f32), 0.0).astype(bf16)
+            coarse_wide[k, :, peer * pd : (peer + 1) * pd] = coarse_all[peer, k]
 
     def turn_over(step, carry):
         k, wide = step % 3, step // 3
-        rank_turned = turn(right[k, :, pl.ds(pl.multiple_of(wide * clq, clq), clq)]).astype(bf16)
+        rank_turned = turn(coarse_wide[k, :, pl.ds(pl.multiple_of(wide * clq, clq), clq)]).astype(bf16)
         for group in range(row_groups):
             span = slice(group * clp, (group + 1) * clp)
-            value = jnp.dot(rank_turned, left[:, span], preferred_element_type=f32)
+            value = jnp.dot(rank_turned, left[km:kt, span], preferred_element_type=f32)
             value = value + turn(dense[span, pl.ds(pl.multiple_of(step * clq, clq), clq)])
             dense_turned[step, :, span] = value.astype(bf16)
         return carry
@@ -274,13 +292,9 @@
             for part in range(per_col):
                 bsend[wide * per_col + part, k] = value[part]
         last = turn_index == col_groups - 1
-        for part in range(per_col):
-            if last:
-                if part == 0:
-                    continue
-                peer = wide * per_col + lax.rem(lax.rem(me_r, per_col) + part, per_col)
-            else:
-                peer = wide * per_col + part
+        for part in range(1 if last else 0, per_col):
+            beside = lax.rem(lax.rem(me_r, per_col) + (part if last else part + 1), per_col)
+            peer = wide * per_col + beside
             post(BACK, {"row": peer}, bsend.at[peer], brecv.at[me_r]).start()
         if turn_index == 0:
             sq[me_r] = fold(gathered.astype(f32))
@@ -293,14 +307,15 @@
     points = pt * n_row * n_col
     beta = jnp.sqrt(jnp.sum(square_sum, axis=0, keepdims=True) / points + tiny_add)
     beta_out[...] = beta
-    u_out[...] = u_old[...] / beta
+    inverse = 1.0 / beta
+    u_out[...] = u_old[...] * inverse
     every(BACK, brecv, n_row).wait_recv()
     v_squares = jnp.zeros((8, rhs), f32)
     for k in range(3):
         total = jnp.zeros((pd, rhs), f32)
         for peer in range(n_row):
             total = total + brecv[peer, k].astype(f32)
-        v_hat = total / beta - beta * v_old[k]
+        v_hat = total * inverse - beta * v_old[k]
         v_out[k] = v_hat
         v_squares = v_squares + fold(v_hat)
     if n_row * n_col <= WHOLE_LIMIT:
@@ -386,9 +401,11 @@
         pltpu.VMEM((1, rhs), f32),
         pltpu.VMEM((kt, row_span), bf16),
         pltpu.VMEM((row_span, kt), bf16),
-        pltpu.VMEM((3, kt, col_span), bf16),
+        pltpu.VMEM((3, km, col_span), bf16),
         pltpu.VMEM((n_row, 3, pd, rhs), bf16),
         pltpu.VMEM((n_row, 3, kc, pd), bf16),
+        pltpu.VMEM((3, kc, col_span), bf16),
+        pltpu.VMEM((row_span, rhs), f32),
         pltpu.VMEM((n_row, kc, rhs), bf16),
         pltpu.VMEM((slots, row_groups * col_groups, rhs), f32),
         pltpu.VMEM((row_span, 3 * col_span), bf16),

time: 32.3 us -> 30.9 us (0.957)
  Pallas kernels: 29.6 us -> 28.2 us
    pallas_call x1, Pallas kernels: 28.9 us -> 27.5 us  [per_device(): pl.pallas_call(functools.partial(kernel, (n_row, n_col)), out_shape=(pltp...]
where the time goes in v4:
time: 30.9 us; the launch traced here: 30.8 us
  Pallas kernels  28.2 us (91%)
  between operations  2.58 us (8%)
    pallas_call x1, Pallas kernels, per_device(): pl.pallas_call(functools.partial(kernel, (n_row, n_col)), out_shape=(pltp...  27.5 us
    pallas_call x1, Pallas kernels, per_device(): pl.pallas_call(functools.partial(finish, 3 * pd * n_row * n_col), out_sha...  0.7 us

profile of v4, /device:TPU:0, one launch (start us, length us, event | category | flops | bytes accessed | tf_op | source)
XLA Modules:
  0.0 30.8 jit_solution(2200541760792457698)
XLA Ops:
  2.6 27.5 %lsqr.1 = (f32[64,128]{1,0:T(8,128)S(1)}, f32[3,64,128]{2,1,0:T(8,128)S(1)}, f32[1,128]{1,0:T(1,128)S(1)}, f32[32,1,128]{2,1,0:T(1,128)S(1)}) custom-call(s32[1,1,16]{2,1,0:T(1,128)} %rows_hbm.1, s32[1,1,16]{2,1,0:T(1,128)} %cols_hbm.1, s32[1,1]{1,0:T(1,128)S(6)} %copy.16.count_hbm, s32[1,1]{1,0:T(1,128)S(6)} %copy.17.mid_rank_hbm, ...), custom_call_target="tpu_custom_call" | custom-call | tf_op jit(solution)/shard_map/lsqr/pallas_call | solution.py:425
  30.0 0.7 %finish.1 = (f32[64,128]{1,0:T(8,128)}, f32[3,64,128]{2,1,0:T(8,128)}, f32[2,128]{1,0:T(2,128)}) custom-call(f32[64,128]{1,0:T(8,128)S(1)} %get-tuple-element.7.u_ref, f32[3,64,128]{2,1,0:T(8,128)S(1)} %get-tuple-element.8.v_ref, f32[1,128]{1,0:T(1,128)S(1)} %get-tuple-element.9.beta_ref, f32[32,1,128]{2,1,0:T(1,128)S(1)} %get-tuple-element.10.squares_ref), custom_call_target="tpu_custom_call" | custom-call | tf_op jit(solution)/shard_map/finish/pallas_call | solution.py:455

commit v5 on v4

--- a/solution.py
+++ b/solution.py
@@ -11,7 +11,7 @@
 MESH = pl.DeviceIdType.MESH
 f32, bf16 = jnp.float32, jnp.bfloat16
 WHOLE_LIMIT = 64
-COARSE, SLIP, SUMS, LEFT, SQUARES, BACK, ALL, COLS, PARTS = range(9)
+COARSE, SLIP, SUMS, LEFT, SQUARES, BACK, ALL, COLS, PARTS, PAIR, BACK_V = range(11)
 
 
 def fold(values):
@@ -68,6 +68,10 @@
     bsend,
     brecv,
     vsq_col,
+    v_pair,
+    v_sent,
+    v_back,
+    spare,
     near_sem,
     in_sem,
     send_sem,
@@ -83,6 +87,8 @@
     row_span, col_span = left.shape[1], right.shape[2]
     row_groups, col_groups = row_span // clp, col_span // clq
     per_col = clq // pd
+    if n_row % 2 or per_col != 2:
+        raise ValueError("uneven mesh")
     spots = row_groups * col_groups
     bunch = 8 if spots % 8 == 0 else spots
     tile = 32
@@ -100,15 +106,13 @@
     else:
         masks = list(range(n_col - 1, 0, -2)) + list(range(n_col - 2, 0, -2))
         col_peers = [flipped(me_c, mask) for mask in masks]
-    if n_row % 2:
-        row_peers = [lax.rem(me_r + step, n_row) for step in range(1, n_row)]
-    else:
-        own_chip, core = me_r // 2, lax.rem(me_r, 2)
-        row_peers = []
-        for step in range(1, n_row // 2):
-            chip = lax.rem(own_chip + step, n_row // 2)
-            row_peers += [chip * 2 + 1 - core, chip * 2 + core]
-        row_peers += [own_chip * 2 + 1 - core]
+    chips = n_row // 2
+    own_chip, lead = me_r // 2, lax.rem(me_r, 2)
+    row_peers = []
+    for step in range(1, chips):
+        chip = lax.rem(own_chip + step, chips)
+        row_peers += [chip * 2 + 1 - lead, chip * 2 + lead]
+    row_peers += [own_chip * 2 + 1 - lead]
 
     loads = [
         pltpu.make_async_copy(src, dst, in_sem.at[place])
@@ -145,8 +149,6 @@
         )
         for piece in range(pieces)
     ]
-    for load in near_loads:
-        load.start()
     for load in loads[2:]:
         load.start()
 
@@ -173,6 +175,8 @@
         return post(place, {"row": row_peers[0]}, buffer.at[pl.ds(0, count - 1)], buffer.at[pl.ds(0, count - 1)])
 
     loads[0].wait()
+    for load in near_loads:
+        load.start()
     slip[me_r] = v_old[...].astype(bf16)
     loads[1].wait()
     own_codes = jnp.zeros((kc, rhs), f32)
@@ -182,6 +186,14 @@
     pl.semaphore_wait(barrier, n_row + n_col - 2)
     across_rows(PARTS, lambda peer: part_codes.at[me_r], part_codes.at[me_r])
     across_rows(SLIP, lambda peer: slip.at[me_r], slip.at[me_r])
+
+    def pair(place, source, target):
+        return post(place, {"row": own_chip * 2 + 1 - lead}, source, target)
+
+    @pl.when(lead == 0)
+    def _():
+        pair(PAIR, v_old, v_pair).start()
+
     for load in loads[2:]:
         load.wait()
     place = lax.broadcasted_iota(jnp.int32, (kt, row_span), 0)
@@ -283,23 +295,27 @@
     every(LEFT, ug, n_col).wait_recv()
 
     gathered = ug[...].reshape(row_span, rhs)
-    own_wide = me_r // per_col
-    for turn_index in range(col_groups):
-        wide = lax.rem(own_wide + 1 + turn_index, col_groups)
+    for step in range(chips):
+        chip = lax.rem(own_chip + 1 + step, chips)
         for k in range(3):
-            value = jnp.dot(dense_turned[wide * 3 + k], gathered, preferred_element_type=f32)
-            value = value.astype(bf16).reshape(per_col, pd, rhs)
-            for part in range(per_col):
-                bsend[wide * per_col + part, k] = value[part]
-        last = turn_index == col_groups - 1
-        for part in range(1 if last else 0, per_col):
-            beside = lax.rem(lax.rem(me_r, per_col) + (part if last else part + 1), per_col)
-            peer = wide * per_col + beside
-            post(BACK, {"row": peer}, bsend.at[peer], brecv.at[me_r]).start()
-        if turn_index == 0:
+            value = jnp.dot(dense_turned[chip * 3 + k], gathered, preferred_element_type=f32)
+            value = value.astype(bf16).reshape(2, pd, rhs)
+            for part in range(2):
+                bsend[chip, part, k] = value[part]
+        if step < chips - 1:
+            post(BACK, {"row": chip * 2 + 1}, bsend.at[chip], brecv.at[me_r]).start()
+        if step == 0:
             sq[me_r] = fold(gathered.astype(f32))
             across_rows(SQUARES, lambda peer: sq.at[me_r], sq.at[me_r])
-    brecv[me_r] = bsend[me_r]
+
+    @pl.when(lead == 0)
+    def _():
+        pair(BACK, bsend.at[own_chip], brecv.at[me_r]).start()
+
+    @pl.when(lead == 1)
+    def _():
+        brecv[me_r] = bsend[own_chip]
+
     every(SQUARES, sq, n_row).wait_recv()
     square_sum = jnp.zeros((8, rhs), f32)
     for peer in range(n_row):
@@ -309,33 +325,52 @@
     beta_out[...] = beta
     inverse = 1.0 / beta
     u_out[...] = u_old[...] * inverse
-    every(BACK, brecv, n_row).wait_recv()
-    v_squares = jnp.zeros((8, rhs), f32)
-    for k in range(3):
-        total = jnp.zeros((pd, rhs), f32)
-        for peer in range(n_row):
-            total = total + brecv[peer, k].astype(f32)
-        v_hat = total * inverse - beta * v_old[k]
-        v_out[k] = v_hat
-        v_squares = v_squares + fold(v_hat)
-    if n_row * n_col <= WHOLE_LIMIT:
-        others = [(a, b) for b in reversed(range(n_col)) for a in reversed(range(n_row))][:-1]
-        own = vsq_all.at[me_c * n_row + me_r]
-        vsq_all[me_c * n_row + me_r] = jnp.sum(v_squares, axis=0, keepdims=True)
-        for a, b in others:
-            post(ALL, (lax.rem(me_r + a, n_row), lax.rem(me_c + b, n_col)), own, own).start()
-        every(ALL, vsq_all, n_row * n_col).wait_recv()
-    else:
-        vsq_col[me_c] = v_squares
-        across_cols(COLS, lambda peer: vsq_col.at[me_c], vsq_col.at[me_c])
-        every(COLS, vsq_col, n_col).wait_recv()
+    whole = n_row * n_col <= WHOLE_LIMIT
+    leads = vsq_all.shape[0]
+
+    @pl.when(lead == 1)
+    def _():
+        pair(PAIR, v_pair, v_pair).wait_recv()
+        every(BACK, brecv, n_row).wait_recv()
         v_squares = jnp.zeros((8, rhs), f32)
-        for peer in range(n_col):
-            v_squares = v_squares + vsq_col[peer]
-        vsq_all[me_r] = v_squares
-        across_rows(ALL, lambda peer: vsq_all.at[me_r], vsq_all.at[me_r])
-        every(ALL, vsq_all, n_row).wait_recv()
-        every(COLS, vsq_col, n_col).wait_send()
+        for part, (old, new) in enumerate([(v_pair, v_sent), (v_old, v_out)]):
+            for k in range(3):
+                total = jnp.zeros((pd, rhs), f32)
+                for peer in range(n_row):
+                    total = total + brecv[peer, part, k].astype(f32)
+                v_hat = total * inverse - beta * old[k]
+                new[k] = v_hat
+                v_squares = v_squares + fold(v_hat)
+        if whole:
+            own = vsq_all.at[me_c * chips + own_chip]
+            vsq_all[me_c * chips + own_chip] = jnp.sum(v_squares, axis=0, keepdims=True)
+            others = [(a, b) for b in reversed(range(n_col)) for a in reversed(range(n_row))][:-1]
+            for a, b in others:
+                post(ALL, (lax.rem(me_r + a, n_row), lax.rem(me_c + b, n_col)), own, own).start()
+        else:
+            vsq_col[me_c] = v_squares
+            across_cols(COLS, lambda peer: vsq_col.at[me_c], vsq_col.at[me_c])
+            every(COLS, vsq_col, n_col).wait_recv()
+            v_squares = jnp.zeros((8, rhs), f32)
+            for peer in range(n_col):
+                v_squares = v_squares + vsq_col[peer]
+            vsq_all[own_chip] = v_squares
+            across_rows(ALL, lambda peer: vsq_all.at[own_chip], vsq_all.at[own_chip])
+            every(COLS, vsq_col, n_col).wait_send()
+        pair(BACK_V, v_sent, v_back).start()
+        every(ALL, vsq_all, leads).wait_recv()
+        every(BACK, bsend, chips).wait_send()
+        pair(BACK_V, v_sent, v_back).wait_send()
+        every(ALL, spare, spare.shape[0]).wait_send()
+
+    @pl.when(lead == 0)
+    def _():
+        pair(BACK_V, v_back, v_back).wait_recv()
+        v_out[...] = v_back[...]
+        every(ALL, vsq_all, leads + 1).wait_recv()
+        pair(PAIR, v_old, v_pair).wait_send()
+        every(BACK, bsend, chips + 1).wait_send()
+
     for place, buffer in (
         (PARTS, part_codes),
         (COARSE, coarse_all),
@@ -343,8 +378,6 @@
         (SUMS, fsend),
         (LEFT, ug),
         (SQUARES, sq),
-        (BACK, bsend),
-        (ALL, vsq_all),
     ):
         every(place, buffer, buffer.shape[0]).wait_send()
 
@@ -388,7 +421,7 @@
     vmem = pl.BlockSpec(memory_space=pltpu.VMEM)
     dma = pltpu.SemaphoreType.DMA
     whole = n_row * n_col <= WHOLE_LIMIT
-    sums = (n_row * n_col, 1, rhs) if whole else (n_row, 8, rhs)
+    sums = (n_row // 2 * n_col, 1, rhs) if whole else (n_row // 2, 8, rhs)
     scratch = [
         pltpu.SMEM(near_rows.shape, jnp.int32),
         pltpu.SMEM(near_cols.shape, jnp.int32),
@@ -414,13 +447,17 @@
         pltpu.VMEM((n_col, pt, rhs), bf16),
         pltpu.VMEM((n_col, pt, rhs), bf16),
         pltpu.VMEM((n_row, 8, rhs), f32),
-        pltpu.VMEM((n_row, 3, pd, rhs), bf16),
-        pltpu.VMEM((n_row, 3, pd, rhs), bf16),
+        pltpu.VMEM((n_row // 2, 2, 3, pd, rhs), bf16),
+        pltpu.VMEM((n_row, 2, 3, pd, rhs), bf16),
         pltpu.VMEM((n_col, 8, rhs), f32),
+        pltpu.VMEM((3, pd, rhs), f32),
+        pltpu.VMEM((3, pd, rhs), f32),
+        pltpu.VMEM((3, pd, rhs), f32),
+        pltpu.VMEM((n_row * n_col, 1, rhs) if whole else (n_row, 8, rhs), f32),
         dma,
         dma((12,)),
-        dma((9,)),
-        dma((9,)),
+        dma((11,)),
+        dma((11,)),
     ]
     held = pl.pallas_call(
         functools.partial(kernel, (n_row, n_col)),

time: 30.9 us -> 30.1 us (0.974)
  Pallas kernels: 28.2 us -> 27.3 us
    pallas_call x1, Pallas kernels: 27.5 us -> 26.6 us  [per_device(): pl.pallas_call(functools.partial(kernel, (n_row, n_col)), out_shape=(pltp...]
where the time goes in v5:
time: 30.1 us; the launch traced here: 29.9 us
  Pallas kernels  27.3 us (91%)
  between operations  2.58 us (9%)
    pallas_call x1, Pallas kernels, per_device(): pl.pallas_call(functools.partial(kernel, (n_row, n_col)), out_shape=(pltp...  26.6 us
    pallas_call x1, Pallas kernels, per_device(): pl.pallas_call(functools.partial(finish, 3 * pd * n_row * n_col), out_sha...  0.69 us

profile of v5, /device:TPU:0, one launch (start us, length us, event | category | flops | bytes accessed | tf_op | source)
XLA Modules:
  0.0 29.9 jit_solution(6384540491481631113)
XLA Ops:
  2.6 26.6 %lsqr.1 = (f32[64,128]{1,0:T(8,128)S(1)}, f32[3,64,128]{2,1,0:T(8,128)S(1)}, f32[1,128]{1,0:T(1,128)S(1)}, f32[16,1,128]{2,1,0:T(1,128)S(1)}) custom-call(s32[1,1,16]{2,1,0:T(1,128)} %rows_hbm.1, s32[1,1,16]{2,1,0:T(1,128)} %cols_hbm.1, s32[1,1]{1,0:T(1,128)S(6)} %copy.16.count_hbm, s32[1,1]{1,0:T(1,128)S(6)} %copy.17.mid_rank_hbm, ...), custom_call_target="tpu_custom_call" | custom-call | tf_op jit(solution)/shard_map/lsqr/pallas_call | solution.py:462
  29.2 0.7 %finish.1 = (f32[64,128]{1,0:T(8,128)}, f32[3,64,128]{2,1,0:T(8,128)}, f32[2,128]{1,0:T(2,128)}) custom-call(f32[64,128]{1,0:T(8,128)S(1)} %get-tuple-element.7.u_ref, f32[3,64,128]{2,1,0:T(8,128)S(1)} %get-tuple-element.8.v_ref, f32[1,128]{1,0:T(1,128)S(1)} %get-tuple-element.9.beta_ref, f32[16,1,128]{2,1,0:T(1,128)S(1)} %get-tuple-element.10.squares_ref), custom_call_target="tpu_custom_call" | custom-call | tf_op jit(solution)/shard_map/finish/pallas_call | solution.py:492

commit v6 on v5

--- a/solution.py
+++ b/solution.py
@@ -76,6 +76,7 @@
     in_sem,
     send_sem,
     recv_sem,
+    known,
 ):
     n_row, n_col = sizes
     me_r, me_c = lax.axis_index("row"), lax.axis_index("col")
@@ -106,6 +107,9 @@
     else:
         masks = list(range(n_col - 1, 0, -2)) + list(range(n_col - 2, 0, -2))
         col_peers = [flipped(me_c, mask) for mask in masks]
+    far_cols = col_peers
+    if not n_col & (n_col - 1):
+        far_cols = [flipped(me_c, mask) for mask in range(n_col - 1, 0, -1)]
     chips = n_row // 2
     own_chip, lead = me_r // 2, lax.rem(me_r, 2)
     row_peers = []
@@ -137,8 +141,11 @@
     loads[1].start()
 
     barrier = pltpu.get_barrier_semaphore()
-    for peer in col_peers:
-        pl.semaphore_signal(barrier, device_id={"col": peer}, device_id_type=MESH)
+    @pl.when(lead == 1)
+    def _():
+        for peer in col_peers:
+            pl.semaphore_signal(barrier, device_id={"col": peer}, device_id_type=MESH)
+
     for peer in row_peers:
         pl.semaphore_signal(barrier, device_id={"row": peer}, device_id_type=MESH)
     pieces = 4 if slots % 4 == 0 else 1
@@ -183,7 +190,7 @@
     for k in range(3):
         own_codes = own_codes + jnp.dot(coarse_all[me_r, k], slip[me_r, k], preferred_element_type=f32)
     part_codes[me_r] = own_codes.astype(bf16)
-    pl.semaphore_wait(barrier, n_row + n_col - 2)
+    pl.semaphore_wait(barrier, n_row - 1 + lead * (n_col - 1))
     across_rows(PARTS, lambda peer: part_codes.at[me_r], part_codes.at[me_r])
     across_rows(SLIP, lambda peer: slip.at[me_r], slip.at[me_r])
 
@@ -193,6 +200,11 @@
     @pl.when(lead == 0)
     def _():
         pair(PAIR, v_old, v_pair).start()
+
+    @pl.when(lead == 1)
+    def _():
+        for peer in col_peers:
+            pl.semaphore_signal(known, device_id={"col": peer}, device_id_type=MESH)
 
     for load in loads[2:]:
         load.wait()
@@ -240,6 +252,12 @@
         return carry
 
     lax.fori_loop(0, spots // bunch * 3 * chunks, build, 0)
+
+    @pl.when(lead == 1)
+    def _():
+        pl.semaphore_wait(known, n_col - 1)
+        pl.semaphore_signal(known, device_id={"row": me_r - 1}, device_id_type=MESH)
+
     across_rows(COARSE, lambda peer: coarse_all.at[me_r], coarse_all.at[me_r])
     every(PARTS, part_codes, n_row).wait_recv()
     coarse_codes = jnp.zeros((kc, rhs), f32)
@@ -265,6 +283,10 @@
         fsend[group * wave // pt : (group + 1) * wave // pt] = value.astype(bf16).reshape(
             wave // pt, pt, rhs
         )
+    @pl.when(lead == 0)
+    def _():
+        pl.semaphore_wait(known, 1)
+
     across_cols(SUMS, lambda peer: fsend.at[peer], frecv.at[me_c])
     frecv[me_c] = fsend[me_c]
 
@@ -325,6 +347,17 @@
     beta_out[...] = beta
     inverse = 1.0 / beta
     u_out[...] = u_old[...] * inverse
+    def sent():
+        for place, buffer in (
+            (PARTS, part_codes),
+            (COARSE, coarse_all),
+            (SLIP, slip),
+            (SUMS, fsend),
+            (LEFT, ug),
+            (SQUARES, sq),
+        ):
+            every(place, buffer, buffer.shape[0]).wait_send()
+
     whole = n_row * n_col <= WHOLE_LIMIT
     leads = vsq_all.shape[0]
 
@@ -344,9 +377,9 @@
         if whole:
             own = vsq_all.at[me_c * chips + own_chip]
             vsq_all[me_c * chips + own_chip] = jnp.sum(v_squares, axis=0, keepdims=True)
-            others = [(a, b) for b in reversed(range(n_col)) for a in reversed(range(n_row))][:-1]
-            for a, b in others:
-                post(ALL, (lax.rem(me_r + a, n_row), lax.rem(me_c + b, n_col)), own, own).start()
+            for col in far_cols + [me_c]:
+                for row in row_peers + ([] if col is me_c else [me_r]):
+                    post(ALL, (row, col), own, own).start()
         else:
             vsq_col[me_c] = v_squares
             across_cols(COLS, lambda peer: vsq_col.at[me_c], vsq_col.at[me_c])
@@ -358,28 +391,20 @@
             across_rows(ALL, lambda peer: vsq_all.at[own_chip], vsq_all.at[own_chip])
             every(COLS, vsq_col, n_col).wait_send()
         pair(BACK_V, v_sent, v_back).start()
-        every(ALL, vsq_all, leads).wait_recv()
         every(BACK, bsend, chips).wait_send()
+        sent()
         pair(BACK_V, v_sent, v_back).wait_send()
         every(ALL, spare, spare.shape[0]).wait_send()
+        every(ALL, vsq_all, leads).wait_recv()
 
     @pl.when(lead == 0)
     def _():
         pair(BACK_V, v_back, v_back).wait_recv()
         v_out[...] = v_back[...]
-        every(ALL, vsq_all, leads + 1).wait_recv()
         pair(PAIR, v_old, v_pair).wait_send()
         every(BACK, bsend, chips + 1).wait_send()
-
-    for place, buffer in (
-        (PARTS, part_codes),
-        (COARSE, coarse_all),
-        (SLIP, slip),
-        (SUMS, fsend),
-        (LEFT, ug),
-        (SQUARES, sq),
-    ):
-        every(place, buffer, buffer.shape[0]).wait_send()
+        sent()
+        every(ALL, vsq_all, leads + 1).wait_recv()
 
 
 def finish(unknowns, u_ref, v_ref, beta_ref, squares_ref, u_out, v_out, norms_out):
@@ -458,6 +483,7 @@
         dma((12,)),
         dma((11,)),
         dma((11,)),
+        pltpu.SemaphoreType.REGULAR,
     ]
     held = pl.pallas_call(
         functools.partial(kernel, (n_row, n_col)),

time: 30.1 us -> 29.8 us (0.990)
    pallas_call x1, Pallas kernels: 26.6 us -> 26.3 us  [per_device(): pl.pallas_call(functools.partial(kernel, (n_row, n_col)), out_shape=(pltp...]
where the time goes in v6:
time: 29.8 us; the launch traced here: 29.6 us
  Pallas kernels  27 us (91%)
  between operations  2.58 us (9%)
    pallas_call x1, Pallas kernels, per_device(): pl.pallas_call(functools.partial(kernel, (n_row, n_col)), out_shape=(pltp...  26.3 us
    pallas_call x1, Pallas kernels, per_device(): pl.pallas_call(functools.partial(finish, 3 * pd * n_row * n_col), out_sha...  0.69 us

profile of v6, /device:TPU:0, one launch (start us, length us, event | category | flops | bytes accessed | tf_op | source)
XLA Modules:
  0.0 29.6 jit_solution(18418127194579195382)
XLA Ops:
  2.6 26.3 %lsqr.1 = (f32[64,128]{1,0:T(8,128)S(1)}, f32[3,64,128]{2,1,0:T(8,128)S(1)}, f32[1,128]{1,0:T(1,128)S(1)}, f32[16,1,128]{2,1,0:T(1,128)S(1)}) custom-call(s32[1,1,16]{2,1,0:T(1,128)} %rows_hbm.1, s32[1,1,16]{2,1,0:T(1,128)} %cols_hbm.1, s32[1,1]{1,0:T(1,128)S(6)} %copy.16.count_hbm, s32[1,1]{1,0:T(1,128)S(6)} %copy.17.mid_rank_hbm, ...), custom_call_target="tpu_custom_call" | custom-call | tf_op jit(solution)/shard_map/lsqr/pallas_call | solution.py:488
  28.9 0.7 %finish.1 = (f32[64,128]{1,0:T(8,128)}, f32[3,64,128]{2,1,0:T(8,128)}, f32[2,128]{1,0:T(2,128)}) custom-call(f32[64,128]{1,0:T(8,128)S(1)} %get-tuple-element.7.u_ref, f32[3,64,128]{2,1,0:T(8,128)S(1)} %get-tuple-element.8.v_ref, f32[1,128]{1,0:T(1,128)S(1)} %get-tuple-element.9.beta_ref, f32[16,1,128]{2,1,0:T(1,128)S(1)} %get-tuple-element.10.squares_ref), custom_call_target="tpu_custom_call" | custom-call | tf_op jit(solution)/shard_map/finish/pallas_call | solution.py:518

commit v7 on v6

--- a/solution.py
+++ b/solution.py
@@ -11,7 +11,7 @@
 MESH = pl.DeviceIdType.MESH
 f32, bf16 = jnp.float32, jnp.bfloat16
 WHOLE_LIMIT = 64
-COARSE, SLIP, SUMS, LEFT, SQUARES, BACK, ALL, COLS, PARTS, PAIR, BACK_V = range(11)
+COARSE, SLIP, SUMS, LEFT, SQUARES, BACK, ALL, COLS, PARTS, PAIR, BACK_V, SLIP_NEAR = range(12)
 
 
 def fold(values):
@@ -192,10 +192,13 @@
     part_codes[me_r] = own_codes.astype(bf16)
     pl.semaphore_wait(barrier, n_row - 1 + lead * (n_col - 1))
     across_rows(PARTS, lambda peer: part_codes.at[me_r], part_codes.at[me_r])
-    across_rows(SLIP, lambda peer: slip.at[me_r], slip.at[me_r])
+    for peer in row_peers[:-1]:
+        post(SLIP, {"row": peer}, slip.at[me_r], slip.at[me_r]).start()
 
     def pair(place, source, target):
         return post(place, {"row": own_chip * 2 + 1 - lead}, source, target)
+
+    pair(SLIP_NEAR, slip.at[me_r], slip.at[me_r]).start()
 
     @pl.when(lead == 0)
     def _():
@@ -268,18 +271,22 @@
     for group in range(row_span // wave):
         span = slice(group * wave, (group + 1) * wave)
         begun[span, :] = jnp.dot(left_turned[span, km:kt], coarse_codes, preferred_element_type=f32)
-    every(SLIP, slip, n_row).wait_recv()
-    gathered = jnp.concatenate(
-        [
-            slip[wide * per_col : (wide + 1) * per_col, k].reshape(clq, rhs)
-            for wide in range(col_groups)
-            for k in range(3)
-        ],
-        axis=0,
-    )
+    pair(SLIP_NEAR, slip.at[me_r], slip.at[me_r]).wait_recv()
+
+    def product(span, chip):
+        held = jnp.concatenate([slip[pl.ds(chip * 2, 2), k].reshape(clq, rhs) for k in range(3)], axis=0)
+        lanes = pl.ds(pl.multiple_of(chip * (3 * clq), 3 * clq), 3 * clq)
+        return jnp.dot(dense[span, lanes], held, preferred_element_type=f32)
+
     for group in range(row_span // wave):
         span = slice(group * wave, (group + 1) * wave)
-        value = begun[span, :] + jnp.dot(dense[span, :], gathered, preferred_element_type=f32)
+        begun[span, :] = begun[span, :] + product(span, own_chip)
+    every(SLIP, slip, n_row - 1).wait_recv()
+    for group in range(row_span // wave):
+        span = slice(group * wave, (group + 1) * wave)
+        value = begun[span, :]
+        for step in range(1, chips):
+            value = value + product(span, lax.rem(own_chip + step, chips))
         fsend[group * wave // pt : (group + 1) * wave // pt] = value.astype(bf16).reshape(
             wave // pt, pt, rhs
         )
@@ -351,12 +358,13 @@
         for place, buffer in (
             (PARTS, part_codes),
             (COARSE, coarse_all),
-            (SLIP, slip),
             (SUMS, fsend),
             (LEFT, ug),
             (SQUARES, sq),
         ):
             every(place, buffer, buffer.shape[0]).wait_send()
+        every(SLIP, slip, n_row - 1).wait_send()
+        pair(SLIP_NEAR, slip.at[me_r], slip.at[me_r]).wait_send()
 
     whole = n_row * n_col <= WHOLE_LIMIT
     leads = vsq_all.shape[0]
@@ -481,8 +489,8 @@
         pltpu.VMEM((n_row * n_col, 1, rhs) if whole else (n_row, 8, rhs), f32),
         dma,
         dma((12,)),
-        dma((11,)),
-        dma((11,)),
+        dma((12,)),
+        dma((12,)),
         pltpu.SemaphoreType.REGULAR,
     ]
     held = pl.pallas_call(

time: 29.8 us -> 29.7 us (level)
  no operation moved by 1% of the time
where the time goes in v7:
time: 29.7 us; the launch traced here: 29.5 us
  Pallas kernels  26.9 us (91%)
  between operations  2.58 us (9%)
    pallas_call x1, Pallas kernels, per_device(): pl.pallas_call(functools.partial(kernel, (n_row, n_col)), out_shape=(pltp...  26.2 us
    pallas_call x1, Pallas kernels, per_device(): pl.pallas_call(functools.partial(finish, 3 * pd * n_row * n_col), out_sha...  0.69 us

profile of v7, /device:TPU:0, one launch (start us, length us, event | category | flops | bytes accessed | tf_op | source)
XLA Modules:
  0.0 29.5 jit_solution(8229173648751245698)
XLA Ops:
  2.6 26.2 %lsqr.1 = (f32[64,128]{1,0:T(8,128)S(1)}, f32[3,64,128]{2,1,0:T(8,128)S(1)}, f32[1,128]{1,0:T(1,128)S(1)}, f32[16,1,128]{2,1,0:T(1,128)S(1)}) custom-call(s32[1,1,16]{2,1,0:T(1,128)} %rows_hbm.1, s32[1,1,16]{2,1,0:T(1,128)} %cols_hbm.1, s32[1,1]{1,0:T(1,128)S(6)} %copy.16.count_hbm, s32[1,1]{1,0:T(1,128)S(6)} %copy.17.mid_rank_hbm, ...), custom_call_target="tpu_custom_call" | custom-call | tf_op jit(solution)/shard_map/lsqr/pallas_call | solution.py:496
  28.8 0.7 %finish.1 = (f32[64,128]{1,0:T(8,128)}, f32[3,64,128]{2,1,0:T(8,128)}, f32[2,128]{1,0:T(2,128)}) custom-call(f32[64,128]{1,0:T(8,128)S(1)} %get-tuple-element.7.u_ref, f32[3,64,128]{2,1,0:T(8,128)S(1)} %get-tuple-element.8.v_ref, f32[1,128]{1,0:T(1,128)S(1)} %get-tuple-element.9.beta_ref, f32[16,1,128]{2,1,0:T(1,128)S(1)} %get-tuple-element.10.squares_ref), custom_call_target="tpu_custom_call" | custom-call | tf_op jit(solution)/shard_map/finish/pallas_call | solution.py:526
